TPU v7x, 32 devices: a whole 2x2x4 slice. The times are simulated.
32 devices in a mesh: cell: 16 (over z, y, x), gene: 2 (over core).
Axes of the slice: x: 2, y: 2, z: 4, core: 2. Of those that a mesh axis runs over, the one named last changes fastest.
Arguments:
- tiles: bfloat16 [2, 1024, 128, 128], P('gene', 'cell'), may hold values from -8 to 8
- tile_row: int32 [2, 1024], P('gene', 'cell'), may hold values from 0 to 7, as said below
- tile_col: int32 [2, 1024], P('gene', 'cell'), may hold values from 0 to 15
- tile_count: int32 [2, 16], P('gene', 'cell'), may hold values from 1 to 64, as said below
- start_basis: bfloat16 [64, 4096], P(None, 'gene'), may hold values from -0.09375 to 0.09375
Outputs:
- basis: bfloat16 [64, 16384], P(None, 'cell')
- loadings: float32 [64, 4096], P(None, ('gene', 'cell'))
Inputs may be any that keep to these rules, and one draw needn't show every extreme that they name: `tile_row`: tile row of each slot, within 0 to 7; the slots of one device name distinct (row, column) pairs. `tile_count`: slots in use; for each index of gene some device uses all 64.
All inputs are finite; a program needn't handle non-finite values.
Results may differ from a plain program's by a relative error of at most 0.018.
Values may be sent and summed in bfloat16 or wider, within the bound.
A program may use at most 64 MiB of HBM per device.

v0:
```python
import functools

import jax
import jax.numpy as jnp
from jax import lax
from jax.experimental import pallas as pl
from jax.experimental.pallas import tpu as pltpu
from jax.sharding import PartitionSpec as P

ROW_BLOCKS = 8
PANEL = 4
MESH = pl.DeviceIdType.MESH
HIGH = lax.Precision.HIGHEST


def split_three(value):
    high = value.astype(jnp.bfloat16)
    rest = value - high.astype(jnp.float32)
    middle = rest.astype(jnp.bfloat16)
    low = (rest - middle.astype(jnp.float32)).astype(jnp.bfloat16)
    return high, middle, low


def inverse_factor(gram):
    width = gram.shape[0]
    shape = (width, 2 * width)
    row = lax.broadcasted_iota(jnp.int32, shape, 0)
    lane = lax.broadcasted_iota(jnp.int32, shape, 1)
    both = jnp.concatenate([jnp.zeros_like(gram), gram], axis=1)
    both = jnp.where(row == lane, 1.0, both)
    pivots = jnp.ones(shape, jnp.float32)
    done = []
    start = 0
    for first in range(0, width, PANEL):
        base = first // 8 * 8
        if base > start:
            done.append((both[: base - start], pivots[: base - start]))
            both = both[base - start :]
            pivots = pivots[base - start :]
            row = row[base - start :]
            start = base
        columns = [
            jnp.broadcast_to(both[:, width + j : width + j + 1], both.shape)
            for j in range(first, first + PANEL)
        ]
        for k in range(PANEL):
            j = first + k
            at = j - start
            pivot = columns[k][at : at + 1]
            factor = jnp.where(row > j, columns[k] * (1.0 / pivot), 0.0)
            pivots = jnp.where(row == j, pivot, pivots)
            both = both - factor * both[at : at + 1]
            for m in range(k + 1, PANEL):
                columns[m] = columns[m] - factor * columns[m][at : at + 1]
    done.append((both, pivots))
    both = jnp.concatenate([piece for piece, _ in done], axis=0)
    pivots = jnp.concatenate([piece for _, piece in done], axis=0)
    return (both * lax.rsqrt(pivots))[:, :width]


def kernel(
    cells, inner, genes, parts,
    table, tiles, start, basis_out, load_out,
    held, dense, mine, theirs, stacked, grams, planes, sums_out, sums_mid, sums_own, sums_in, middle, basis,
    tile_sem, pair_send, pair_recv, gram_send, gram_recv, plane_send, plane_recv,
    near_send, near_recv, far_send, far_recv, mid_send, mid_recv,
):
    cell = lax.axis_index("cell")
    gene = lax.axis_index("gene")
    slots, side, _ = tiles.shape
    width = start.shape[0]
    cell_dev, gene_dev = dense.shape
    gene_blocks = gene_dev // side
    chunk = gene_dev // cells
    piece = cell_dev // parts
    half = width // 2
    outer = cells // inner
    here = cell // inner
    spot = lax.rem(cell, inner)
    other = lax.rem(gene + 1, genes)

    fetch = pltpu.make_async_copy(tiles, held.at[pl.ds(0, slots)], tile_sem)
    fetch.start()

    barrier = pltpu.get_barrier_semaphore()

    def greet(k, _):
        pl.semaphore_signal(
            barrier, inc=1, device_id={"cell": lax.rem(cell + k, cells)}, device_id_type=MESH
        )
        return 0

    pl.semaphore_signal(barrier, inc=1, device_id={"gene": other}, device_id_type=MESH)
    lax.fori_loop(1, cells, greet, 0)
    held[slots] = jnp.zeros((side, side), held.dtype)
    fetch.wait()

    def place(i, _):
        row = i // gene_blocks
        col = lax.rem(i, gene_blocks)
        dense[
            pl.ds(pl.multiple_of(row * side, side), side),
            pl.ds(pl.multiple_of(col * side, side), side),
        ] = held[table[i]]
        return 0

    lax.fori_loop(0, (cell_dev // side) * gene_blocks, place, 0)
    basis[...] = start[...]
    pl.semaphore_wait(barrier, cells)

    def pair_copy(it, r):
        return pltpu.make_async_remote_copy(
            src_ref=mine.at[it, r], dst_ref=theirs.at[it, r],
            send_sem=pair_send.at[it, r], recv_sem=pair_recv.at[it, r],
            device_id={"gene": other}, device_id_type=MESH,
        )

    def near(k):
        return here * inner + lax.rem(spot + k, inner)

    def far(k):
        return lax.rem(here + k, outer) * inner + spot

    def gram_copy(it, source, k):
        return pltpu.make_async_remote_copy(
            src_ref=grams.at[it, source], dst_ref=grams.at[it, source],
            send_sem=gram_send.at[it, k], recv_sem=gram_recv.at[it, source],
            device_id={"cell": near(k)}, device_id_type=MESH,
        )

    def plane_copy(it, source, k):
        return pltpu.make_async_remote_copy(
            src_ref=planes.at[it, source], dst_ref=planes.at[it, source],
            send_sem=plane_send.at[it, k], recv_sem=plane_recv.at[it, source],
            device_id={"cell": far(k)}, device_id_type=MESH,
        )

    def near_copy(it, group, source, k):
        return pltpu.make_async_remote_copy(
            src_ref=sums_out.at[it, group, lax.rem(spot + k, inner)],
            dst_ref=sums_mid.at[it, group, source],
            send_sem=near_send.at[it, group, k], recv_sem=near_recv.at[it, group, source],
            device_id={"cell": near(k)}, device_id_type=MESH,
        )

    def far_copy(it, source, k):
        return pltpu.make_async_remote_copy(
            src_ref=sums_own.at[it, lax.rem(here + k, outer)], dst_ref=sums_in.at[it, source],
            send_sem=far_send.at[it, k], recv_sem=far_recv.at[it, source],
            device_id={"cell": far(k)}, device_id_type=MESH,
        )

    def mid_copy(source, k):
        return pltpu.make_async_remote_copy(
            src_ref=middle.at[source], dst_ref=middle.at[source],
            send_sem=mid_send.at[k], recv_sem=mid_recv.at[source],
            device_id={"cell": lax.rem(cell + k, cells)}, device_id_type=MESH,
        )

    def each(act):
        def body(k, _):
            act(lax.rem(cell + cells - k, cells), k)
            return 0

        lax.fori_loop(1, cells, body, 0)

    def each_near(act):
        for k in range(1, inner):
            act(lax.rem(spot + inner - k, inner), k)

    def each_far(act):
        for k in range(1, outer):
            act(lax.rem(here + outer - k, outer), k)

    def added(ref, count):
        total = ref[0]
        for c in range(1, count):
            total = total + ref[c]
        return total

    def loop(first, last, act):
        def body(k, _):
            act(k)
            return 0

        lax.fori_loop(first, last, body, 0)

    def part(r):
        return pl.ds(pl.multiple_of(r * piece, piece), piece)

    def iteration(it):
        def score(r):
            mine[it, r] = lax.dot_general(
                basis[...], dense[part(r), :], (((1,), (1,)), ((), ())),
                preferred_element_type=jnp.float32,
            )
            pair_copy(it, r).start()

        def merge(r):
            pair_copy(it, r).wait_recv()
            high, mid, low = split_three(mine[it, r] + theirs[it, r])
            stacked[0:width, part(r)] = high
            stacked[width : 2 * width, part(r)] = mid
            stacked[2 * width : 3 * width, part(r)] = low

        loop(0, parts, score)
        loop(0, parts, merge)

        whole = stacked[...]
        cross = lax.dot_general(
            whole, whole, (((1,), (1,)), ((), ())), preferred_element_type=jnp.float32
        )
        cross = cross[:width] + cross[width : 2 * width] + cross[2 * width :]
        gram = cross[:, :width] + cross[:, width : 2 * width] + cross[:, 2 * width :]
        grams[it, spot] = jnp.concatenate([gram[:half], gram[half:]], axis=1)
        each_near(lambda _, k: gram_copy(it, spot, k).start())

        def product(columns):
            pair = jnp.dot(
                stacked[0 : 2 * width, :], columns, preferred_element_type=jnp.float32
            )
            return pair[:width] + pair[width:]

        span = inner * chunk

        def multiply(k):
            group = lax.rem(here + k, outer)
            if span % 128 == 0:
                wide = product(dense[:, pl.ds(pl.multiple_of(group * span, 128), span)])
                for c in range(inner):
                    sums_out[it, group, c] = wide[:, c * chunk : (c + 1) * chunk]
            each_near(lambda _, k: near_copy(it, group, spot, k).start())

        def forward(k):
            group = lax.rem(here + k, outer)
            each_near(lambda source, k: near_copy(it, group, source, k).wait_recv())
            total = sums_out[it, group, spot]
            for c in range(1, inner):
                total = total + sums_mid[it, group, lax.rem(spot + c, inner)]
            if isinstance(k, int):
                sums_in[it, here] = total
            else:
                sums_own[it, group] = total
                far_copy(it, here, k).start()

        if span % 128 != 0:
            for b in range(gene_blocks):
                wide = product(dense[:, b * side : (b + 1) * side])
                for c in range(side // chunk):
                    at = b * (side // chunk) + c
                    sums_out[it, at // inner, at % inner] = wide[:, c * chunk : (c + 1) * chunk]
        multiply(1)
        each_near(lambda source, k: gram_copy(it, source, k).wait_recv())
        planes[it, here] = added(grams.at[it], inner)
        each_far(lambda _, k: plane_copy(it, here, k).start())
        loop(2, outer + 1, multiply)
        loop(1, outer, forward)
        each_far(lambda source, k: plane_copy(it, source, k).wait_recv())
        total = added(planes.at[it], outer)
        total = jnp.concatenate([total[:, :width], total[:, width:]], axis=0)
        inverse = inverse_factor(total)

        @pl.when(it == 1)
        def _():
            scale = jnp.sqrt(jnp.float32(cells * cell_dev))

            def finish(r):
                basis_out[:, part(r)] = (
                    jnp.dot(
                        inverse, mine[it, r] + theirs[it, r], precision=HIGH,
                        preferred_element_type=jnp.float32,
                    ) * scale
                ).astype(basis_out.dtype)

            loop(0, parts, finish)

        forward(0)
        each_far(lambda source, k: far_copy(it, source, k).wait_recv())
        summed = added(sums_in.at[it], outer)
        result = jnp.dot(inverse, summed, precision=HIGH, preferred_element_type=jnp.float32)

        @pl.when(it == 0)
        def _():
            middle[cell] = result.astype(middle.dtype)
            each(lambda _, k: mid_copy(cell, k).start())
            each(lambda source, k: mid_copy(source, k).wait_recv())
            basis[...] = jnp.concatenate([middle[c] for c in range(cells)], axis=1)

        @pl.when(it == 1)
        def _():
            load_out[...] = result

    loop(0, 2, iteration)

    def drain(it):
        loop(0, parts, lambda r: pair_copy(it, r).wait_send())
        each_near(lambda _, k: gram_copy(it, spot, k).wait_send())
        each_far(lambda _, k: plane_copy(it, here, k).wait_send())
        loop(0, outer, lambda group: each_near(lambda _, k: near_copy(it, group, spot, k).wait_send()))
        each_far(lambda _, k: far_copy(it, here, k).wait_send())

    loop(0, 2, drain)
    each(lambda _, k: mid_copy(cell, k).wait_send())


def local(cells, genes, tiles, tile_row, tile_col, tile_count, start_basis):
    slots, side = tiles.shape[1], tiles.shape[-1]
    width, gene_dev = start_basis.shape
    gene_blocks = gene_dev // side
    cell_dev = ROW_BLOCKS * side
    chunk = gene_dev // cells
    parts = 4
    inner = 1
    while inner * inner * 4 <= cells and cells % (inner * 2) == 0:
        inner = inner * 2
    outer = cells // inner
    places = ROW_BLOCKS * gene_blocks
    live = jnp.arange(slots) < tile_count[0, 0]
    spot = jnp.where(live, tile_row[0] * gene_blocks + tile_col[0], places)
    table = jnp.min(
        jnp.where(spot[None, :] == jnp.arange(places)[:, None], jnp.arange(slots)[None, :], slots),
        axis=1,
    ).astype(jnp.int32)
    dma = pltpu.SemaphoreType.DMA
    return pl.pallas_call(
        functools.partial(kernel, cells, inner, genes, parts),
        out_shape=(
            jax.ShapeDtypeStruct((width, cell_dev), jnp.bfloat16),
            jax.ShapeDtypeStruct((width, chunk), jnp.float32),
        ),
        in_specs=[
            pl.BlockSpec(memory_space=pltpu.SMEM),
            pl.BlockSpec(memory_space=pl.ANY),
            pl.BlockSpec(memory_space=pltpu.VMEM),
        ],
        out_specs=(
            pl.BlockSpec(memory_space=pltpu.VMEM),
            pl.BlockSpec(memory_space=pltpu.VMEM),
        ),
        scratch_shapes=[
            pltpu.VMEM((slots + 1, side, side), jnp.bfloat16),
            pltpu.VMEM((cell_dev, gene_dev), jnp.bfloat16),
            pltpu.VMEM((2, parts, width, cell_dev // parts), jnp.float32),
            pltpu.VMEM((2, parts, width, cell_dev // parts), jnp.float32),
            pltpu.VMEM((3 * width, cell_dev), jnp.bfloat16),
            pltpu.VMEM((2, inner, width // 2, 2 * width), jnp.float32),
            pltpu.VMEM((2, outer, width // 2, 2 * width), jnp.float32),
            pltpu.VMEM((2, outer, inner, width, chunk), jnp.float32),
            pltpu.VMEM((2, outer, inner, width, chunk), jnp.float32),
            pltpu.VMEM((2, outer, width, chunk), jnp.float32),
            pltpu.VMEM((2, outer, width, chunk), jnp.float32),
            pltpu.VMEM((cells, width, chunk), jnp.bfloat16),
            pltpu.VMEM((width, gene_dev), jnp.bfloat16),
            dma,
            dma((2, parts)), dma((2, parts)),
            dma((2, inner)), dma((2, inner)), dma((2, outer)), dma((2, outer)),
            dma((2, outer, inner)), dma((2, outer, inner)), dma((2, outer)), dma((2, outer)),
            dma((cells,)), dma((cells,)),
        ],
        compiler_params=pltpu.CompilerParams(
            collective_id=0, has_side_effects=True, vmem_limit_bytes=60 * 1024 * 1024
        ),
    )(table, tiles[0], start_basis)


def solution(mesh):
    return jax.shard_map(
        functools.partial(local, mesh.shape["cell"], mesh.shape["gene"]),
        mesh=mesh,
        in_specs=(
            P("gene", "cell", None, None),
            P("gene", "cell"),
            P("gene", "cell"),
            P("gene", "cell"),
            P(None, "gene"),
        ),
        out_specs=(P(None, "cell"), P(None, ("gene", "cell"))),
        check_vma=False,
    )
```

profile of v0, /device:TPU:0, one launch (start us, length us, event | category | flops | bytes accessed | tf_op | source)
XLA Modules:
  0.0 52.9 jit_solution(13710874688166366887)
XLA Ops:
  1.3 0.7 %fusion = s32[64]{0:T(128)S(1)} fusion(s32[1,64]{1,0:T(1,128)} %param.7, s32[1,64]{1,0:T(1,128)} %param.6, s32[]{:T(128)} %bitcast.4), kind=kLoop, calls=%fused_computation.3 | loop fusion | flops 256 | bytes 772 | tf_op jit(solution)/shard_map/eq | solution.py:321
  2.0 0.6 %select_reduce_fusion.table = s32[128]{0:T(128)} fusion(s32[64]{0:T(128)S(1)} %fusion), kind=kLoop, calls=%fused_computation | loop fusion | flops 24448 | bytes 768 | tf_op jit(solution)/shard_map/reduce_min | solution.py:320
  2.6 47.4 %shard_map.68 = (bf16[64,1024]{1,0:T(8,128)(2,1)}, f32[64,128]{1,0:T(8,128)}) custom-call(s32[128]{0:T(128)} %select_reduce_fusion.table, bf16[64,128,128]{2,1,0:T(8,128)(2,1)} %bitcast.5, bf16[64,2048]{1,0:T(8,128)(2,1)} %start.1), custom_call_target="tpu_custom_call" | custom-call | tf_op jit(solution)/shard_map/pallas_call | solution.py:325
  50.0 1.6 %copy.10 = bf16[64,1024]{1,0:T(8,128)(2,1)} copy(bf16[64,1024]{1,0:T(8,128)(2,1)} %get-tuple-element.4) | data formatting | bytes 262144
  51.5 1.4 %copy.11 = f32[64,128]{1,0:T(8,128)} copy(f32[64,128]{1,0:T(8,128)} %get-tuple-element.5) | data formatting | bytes 65536
where the time goes:
time: 53.2 us; the launch traced here: 52.9 us
  Pallas kernels  47.4 us (89%)
  local copies, waits for them, and re-layouts  2.94 us (6%)
  between operations  1.29 us (2%)
  other arithmetic  1.28 us (2%)
    pallas_call x1, Pallas kernels, local(): pl.pallas_call(functools.partial(kernel, cells, inner, genes, parts), out...  47.4 us
    unnamed x2, local copies, waits for them, and re-layouts  2.94 us

commit v1 on v0

--- a/solution.py
+++ b/solution.py
@@ -31,6 +31,14 @@
     pivots = jnp.ones(shape, jnp.float32)
     done = []
     start = 0
+
+    def spread(first):
+        return {
+            j: jnp.broadcast_to(both[:, width + j : width + j + 1], both.shape)
+            for j in range(first, min(first + PANEL, width))
+        }
+
+    ahead = spread(0)
     for first in range(0, width, PANEL):
         base = first // 8 * 8
         if base > start:
@@ -38,20 +46,20 @@
             both = both[base - start :]
             pivots = pivots[base - start :]
             row = row[base - start :]
+            ahead = {j: column[base - start :] for j, column in ahead.items()}
             start = base
-        columns = [
-            jnp.broadcast_to(both[:, width + j : width + j + 1], both.shape)
-            for j in range(first, first + PANEL)
-        ]
-        for k in range(PANEL):
-            j = first + k
+        columns = ahead
+        ahead = spread(first + PANEL)
+        for j in range(first, first + PANEL):
             at = j - start
-            pivot = columns[k][at : at + 1]
-            factor = jnp.where(row > j, columns[k] * (1.0 / pivot), 0.0)
+            column = columns.pop(j)
+            pivot = column[at : at + 1]
+            factor = jnp.where(row > j, column * (1.0 / pivot), 0.0)
             pivots = jnp.where(row == j, pivot, pivots)
             both = both - factor * both[at : at + 1]
-            for m in range(k + 1, PANEL):
-                columns[m] = columns[m] - factor * columns[m][at : at + 1]
+            for later in (columns, ahead):
+                for m in later:
+                    later[m] = later[m] - factor * later[m][at : at + 1]
     done.append((both, pivots))
     both = jnp.concatenate([piece for piece, _ in done], axis=0)
     pivots = jnp.concatenate([piece for _, piece in done], axis=0)
@@ -60,9 +68,9 @@
 
 def kernel(
     cells, inner, genes, parts,
-    table, tiles, start, basis_out, load_out,
-    held, dense, mine, theirs, stacked, grams, planes, sums_out, sums_mid, sums_own, sums_in, middle, basis,
-    tile_sem, pair_send, pair_recv, gram_send, gram_recv, plane_send, plane_recv,
+    slot_count, slot_row, slot_col, tiles, start, basis_out, load_out,
+    rows_in, cols_in, places_out, table, held, dense, mine, theirs, stacked, grams, planes, sums_out, sums_mid, sums_own, sums_in, middle, basis,
+    tile_sem, slot_sem, table_sem, start_sem, pair_send, pair_recv, gram_send, gram_recv, plane_send, plane_recv,
     near_send, near_recv, far_send, far_recv, mid_send, mid_recv,
 ):
     cell = lax.axis_index("cell")
@@ -79,8 +87,16 @@
     spot = lax.rem(cell, inner)
     other = lax.rem(gene + 1, genes)
 
+    slot_copies = [
+        pltpu.make_async_copy(slot_row, rows_in, slot_sem.at[0]),
+        pltpu.make_async_copy(slot_col, cols_in, slot_sem.at[1]),
+    ]
+    for copy in slot_copies:
+        copy.start()
     fetch = pltpu.make_async_copy(tiles, held.at[pl.ds(0, slots)], tile_sem)
     fetch.start()
+    first_basis = pltpu.make_async_copy(start, basis, start_sem)
+    first_basis.start()
 
     barrier = pltpu.get_barrier_semaphore()
 
@@ -93,19 +109,35 @@
     pl.semaphore_signal(barrier, inc=1, device_id={"gene": other}, device_id_type=MESH)
     lax.fori_loop(1, cells, greet, 0)
     held[slots] = jnp.zeros((side, side), held.dtype)
+    for copy in slot_copies:
+        copy.wait()
+    places = (cell_dev // side) * gene_blocks
+    lane = lax.broadcasted_iota(jnp.int32, (1, slots), 1)
+    spots = jnp.where(lane < slot_count[0, 0], rows_in[...] * gene_blocks + cols_in[...], places)
+    square = (slots, slots)
+    turned = jnp.where(
+        lax.broadcasted_iota(jnp.int32, square, 0) == lax.broadcasted_iota(jnp.int32, square, 1),
+        jnp.broadcast_to(spots, square), 0,
+    )
+    turned = jnp.sum(turned, axis=1, keepdims=True)
+    flat = (slots, places)
+    found = jnp.broadcast_to(turned, flat) == lax.broadcasted_iota(jnp.int32, flat, 1)
+    found = jnp.where(found, lax.broadcasted_iota(jnp.int32, flat, 0), slots)
+    places_out[...] = jnp.min(found, axis=0, keepdims=True)
+    listing = pltpu.make_async_copy(places_out, table, table_sem)
+    listing.start()
+    listing.wait()
     fetch.wait()
 
-    def place(i, _):
-        row = i // gene_blocks
-        col = lax.rem(i, gene_blocks)
-        dense[
-            pl.ds(pl.multiple_of(row * side, side), side),
-            pl.ds(pl.multiple_of(col * side, side), side),
-        ] = held[table[i]]
+    def place(row, _):
+        for col in range(gene_blocks):
+            dense[
+                pl.ds(pl.multiple_of(row * side, side), side), col * side : (col + 1) * side
+            ] = held[table[0, row * gene_blocks + col]]
         return 0
 
-    lax.fori_loop(0, (cell_dev // side) * gene_blocks, place, 0)
-    basis[...] = start[...]
+    lax.fori_loop(0, cell_dev // side, place, 0)
+    first_basis.wait()
     pl.semaphore_wait(barrier, cells)
 
     def pair_copy(it, r):
@@ -163,6 +195,9 @@
             return 0
 
         lax.fori_loop(1, cells, body, 0)
+
+    def farther(k):
+        return lax.rem(k + cells // 2, cells)
 
     def each_near(act):
         for k in range(1, inner):
@@ -315,12 +350,6 @@
         inner = inner * 2
     outer = cells // inner
     places = ROW_BLOCKS * gene_blocks
-    live = jnp.arange(slots) < tile_count[0, 0]
-    spot = jnp.where(live, tile_row[0] * gene_blocks + tile_col[0], places)
-    table = jnp.min(
-        jnp.where(spot[None, :] == jnp.arange(places)[:, None], jnp.arange(slots)[None, :], slots),
-        axis=1,
-    ).astype(jnp.int32)
     dma = pltpu.SemaphoreType.DMA
     return pl.pallas_call(
         functools.partial(kernel, cells, inner, genes, parts),
@@ -330,14 +359,20 @@
         ),
         in_specs=[
             pl.BlockSpec(memory_space=pltpu.SMEM),
-            pl.BlockSpec(memory_space=pl.ANY),
-            pl.BlockSpec(memory_space=pltpu.VMEM),
+            pl.BlockSpec(memory_space=pltpu.HBM),
+            pl.BlockSpec(memory_space=pltpu.HBM),
+            pl.BlockSpec(memory_space=pltpu.HBM),
+            pl.BlockSpec(memory_space=pltpu.HBM),
         ],
         out_specs=(
             pl.BlockSpec(memory_space=pltpu.VMEM),
             pl.BlockSpec(memory_space=pltpu.VMEM),
         ),
         scratch_shapes=[
+            pltpu.VMEM((1, slots), jnp.int32),
+            pltpu.VMEM((1, slots), jnp.int32),
+            pltpu.VMEM((1, places), jnp.int32),
+            pltpu.SMEM((1, places), jnp.int32),
             pltpu.VMEM((slots + 1, side, side), jnp.bfloat16),
             pltpu.VMEM((cell_dev, gene_dev), jnp.bfloat16),
             pltpu.VMEM((2, parts, width, cell_dev // parts), jnp.float32),
@@ -351,16 +386,19 @@
             pltpu.VMEM((2, outer, width, chunk), jnp.float32),
             pltpu.VMEM((cells, width, chunk), jnp.bfloat16),
             pltpu.VMEM((width, gene_dev), jnp.bfloat16),
-            dma,
+            dma, dma((2,)), dma, dma,
             dma((2, parts)), dma((2, parts)),
             dma((2, inner)), dma((2, inner)), dma((2, outer)), dma((2, outer)),
             dma((2, outer, inner)), dma((2, outer, inner)), dma((2, outer)), dma((2, outer)),
             dma((cells,)), dma((cells,)),
         ],
         compiler_params=pltpu.CompilerParams(
-            collective_id=0, has_side_effects=True, vmem_limit_bytes=60 * 1024 * 1024
+            collective_id=0, has_side_effects=True, vmem_limit_bytes=36 * 1024 * 1024
         ),
-    )(table, tiles[0], start_basis)
+    )(tile_count, *(
+        pltpu.with_memory_space_constraint(array, pltpu.HBM)
+        for array in (tile_row, tile_col, tiles[0], start_basis)
+    ))
 
 
 def solution(mesh):

time: 53.2 us -> 48.5 us (0.912)
  local copies, waits for them, and re-layouts: 2.94 us -> 1.27 us
  Pallas kernels: 47.4 us -> 45.8 us
  other arithmetic: 1.28 us -> 0 us
    unnamed x2, local copies, waits for them, and re-layouts: 2.94 us -> 1.27 us
    pallas_call x1, Pallas kernels: 47.4 us -> 45.8 us  [local(): pl.pallas_call(functools.partial(kernel, cells, inner, genes, parts), out...]
    eq x1 -> x0, other arithmetic: 0.68 us -> none  [local(): spot[None, :] == jnp.arange(places)[:, None]]
    reduce_min x1 -> x0, other arithmetic: 0.6 us -> none  [local(): jnp.min(jnp.where(spot[None, :] == jnp.arange(places)[:, None], jnp.arang...]
where the time goes in v1:
time: 48.5 us; the launch traced here: 48.3 us
  Pallas kernels  45.8 us (94%)
  between operations  1.29 us (3%)
  local copies, waits for them, and re-layouts  1.27 us (3%)
    pallas_call x1, Pallas kernels, local(): pl.pallas_call(functools.partial(kernel, cells, inner, genes, parts), out...  45.8 us
    unnamed x2, local copies, waits for them, and re-layouts  1.27 us

profile of v1, /device:TPU:0, one launch (start us, length us, event | category | flops | bytes accessed | tf_op | source)
XLA Modules:
  0.0 48.3 jit_solution(16297825732155404951)
XLA Ops:
  1.3 45.8 %shard_map.68 = (bf16[64,1024]{1,0:T(8,128)(2,1)S(1)}, f32[64,128]{1,0:T(8,128)S(1)}) custom-call(s32[1,1]{1,0:T(1,128)S(6)} %copy.9.slot_count, s32[1,64]{1,0:T(1,128)} %slot_row.1, s32[1,64]{1,0:T(1,128)} %slot_col.1, bf16[64,128,128]{2,1,0:T(8,128)(2,1)} %bitcast.1, bf16[64,2048]{1,0:T(8,128)(2,1)} %start.1), custom_call_target="tpu_custom_call" | custom-call | tf_op jit(solution)/shard_map/pallas_call | solution.py:354
  47.1 0.7 %copy.10 = bf16[64,1024]{1,0:T(8,128)(2,1)} copy(bf16[64,1024]{1,0:T(8,128)(2,1)S(1)} %get-tuple-element.4) | data formatting | bytes 262144
  47.7 0.6 %copy.11 = f32[64,128]{1,0:T(8,128)} copy(f32[64,128]{1,0:T(8,128)S(1)} %get-tuple-element.5) | data formatting | bytes 65536

commit v2 on v1

v2 whole, which is shorter than its diff:
```python
import functools

import jax
import jax.numpy as jnp
from jax import lax
from jax.experimental import pallas as pl
from jax.experimental.pallas import tpu as pltpu
from jax.sharding import PartitionSpec as P

ROW_BLOCKS = 8
PANEL = 4
LEVELS = 32766.0
MESH = pl.DeviceIdType.MESH
HIGH = lax.Precision.HIGHEST
scope = jax.named_scope


def split_three(value):
    high = value.astype(jnp.bfloat16)
    rest = value - high.astype(jnp.float32)
    middle = rest.astype(jnp.bfloat16)
    low = (rest - middle.astype(jnp.float32)).astype(jnp.bfloat16)
    return high, middle, low


def inverse_factor(gram):
    width = gram.shape[0]
    shape = (width, 2 * width)
    row = lax.broadcasted_iota(jnp.int32, shape, 0)
    lane = lax.broadcasted_iota(jnp.int32, shape, 1)
    both = jnp.concatenate([jnp.zeros_like(gram), gram], axis=1)
    both = jnp.where(row == lane, 1.0, both)
    pivots = jnp.ones(shape, jnp.float32)
    done = []
    start = 0

    def spread(first):
        return {
            j: jnp.broadcast_to(both[:, width + j : width + j + 1], both.shape)
            for j in range(first, min(first + PANEL, width))
        }

    ahead = spread(0)
    for first in range(0, width, PANEL):
        base = first // 8 * 8
        if base > start:
            done.append((both[: base - start], pivots[: base - start]))
            both = both[base - start :]
            pivots = pivots[base - start :]
            row = row[base - start :]
            ahead = {j: column[base - start :] for j, column in ahead.items()}
            start = base
        columns = ahead
        ahead = spread(first + PANEL)
        for j in range(first, first + PANEL):
            at = j - start
            column = columns.pop(j)
            pivot = column[at : at + 1]
            factor = jnp.where(row > j, column * (1.0 / pivot), 0.0)
            pivots = jnp.where(row == j, pivot, pivots)
            both = both - factor * both[at : at + 1]
            for later in (columns, ahead):
                for m in later:
                    later[m] = later[m] - factor * later[m][at : at + 1]
    done.append((both, pivots))
    both = jnp.concatenate([piece for piece, _ in done], axis=0)
    pivots = jnp.concatenate([piece for _, piece in done], axis=0)
    return (both * lax.rsqrt(pivots))[:, :width]


def diagonal(width):
    square = (width, width)
    return lax.broadcasted_iota(jnp.int32, square, 0) == lax.broadcasted_iota(jnp.int32, square, 1)


def encode(value):
    peak = jnp.max(jnp.abs(value), axis=1, keepdims=True)
    step = jnp.maximum(peak, 1e-30) * (1.0 / LEVELS)
    coded = jnp.round(value * (1.0 / step)).astype(jnp.int32).astype(jnp.int16)
    square = (value.shape[0], value.shape[0])
    turned = jnp.where(diagonal(square[0]), jnp.broadcast_to(step, square), 0.0)
    return coded, jnp.sum(turned, axis=0, keepdims=True)


def decode(coded, steps):
    square = (coded.shape[0], coded.shape[0])
    turned = jnp.where(diagonal(square[0]), jnp.broadcast_to(steps, square), 0.0)
    step = jnp.sum(turned, axis=1, keepdims=True)
    return coded.astype(jnp.int32).astype(jnp.float32) * step


def kernel(
    cells, inner, genes, parts,
    slot_count, slot_row, slot_col, tiles, start, basis_out, load_out,
    rows_in, cols_in, places_out, table, held, dense, first, mine, theirs, stacked, grams, planes, totals,
    sums_near, codes_out, codes_in, steps_out, steps_in, sums_own, sums_in, middle,
    tile_sem, slot_sem, table_sem, start_sem, pair_send, pair_recv,
    gram_send, gram_recv, plane_send, plane_recv, total_send, total_recv,
    near_send, near_recv, step_send, step_recv, far_send, far_recv, mid_send, mid_recv,
):
    cell = lax.axis_index("cell")
    gene = lax.axis_index("gene")
    slots, side, _ = tiles.shape
    width = start.shape[0]
    cell_dev, gene_dev = dense.shape
    gene_blocks = gene_dev // side
    chunk = gene_dev // cells
    piece = cell_dev // parts
    half = width // 2
    outer = cells // inner
    span = inner * chunk
    here = cell // inner
    spot = lax.rem(cell, inner)
    other = lax.rem(gene + 1, genes)
    lead = gene == genes - 1

    slot_copies = [
        pltpu.make_async_copy(slot_row, rows_in, slot_sem.at[0]),
        pltpu.make_async_copy(slot_col, cols_in, slot_sem.at[1]),
    ]
    for copy in slot_copies:
        copy.start()
    fetch = pltpu.make_async_copy(tiles, held.at[pl.ds(0, slots)], tile_sem)
    fetch.start()
    first_basis = pltpu.make_async_copy(start, first, start_sem)
    first_basis.start()

    barrier = pltpu.get_barrier_semaphore()

    def greet(k, _):
        pl.semaphore_signal(
            barrier, inc=1, device_id={"cell": lax.rem(cell + k, cells)}, device_id_type=MESH
        )
        return 0

    pl.semaphore_signal(barrier, inc=1, device_id={"gene": other}, device_id_type=MESH)
    lax.fori_loop(1, cells, greet, 0)
    held[slots] = jnp.zeros((side, side), held.dtype)
    for copy in slot_copies:
        copy.wait()
    places = (cell_dev // side) * gene_blocks
    lane = lax.broadcasted_iota(jnp.int32, (1, slots), 1)
    spots = jnp.where(
        lane < slot_count[0, 0], rows_in[...] * gene_blocks + cols_in[...], places
    )
    square = (slots, slots)
    turned = jnp.where(diagonal(slots), jnp.broadcast_to(spots, square), 0)
    turned = jnp.sum(turned, axis=1, keepdims=True)
    flat = (slots, places)
    found = jnp.broadcast_to(turned, flat) == lax.broadcasted_iota(jnp.int32, flat, 1)
    found = jnp.where(found, lax.broadcasted_iota(jnp.int32, flat, 0), slots)
    places_out[...] = jnp.min(found, axis=0, keepdims=True)
    listing = pltpu.make_async_copy(places_out, table, table_sem)
    listing.start()
    listing.wait()
    fetch.wait()
    first_basis.wait()

    def pair_copy(it, r):
        return pltpu.make_async_remote_copy(
            src_ref=mine.at[it, r], dst_ref=theirs.at[it, r],
            send_sem=pair_send.at[it, r], recv_sem=pair_recv.at[it, r],
            device_id={"gene": other}, device_id_type=MESH,
        )

    def near(k):
        return here * inner + lax.rem(spot + k, inner)

    def far(k):
        return lax.rem(here + k, outer) * inner + spot

    def gram_copy(it, source, k):
        return pltpu.make_async_remote_copy(
            src_ref=grams.at[it, source], dst_ref=grams.at[it, source],
            send_sem=gram_send.at[it, k], recv_sem=gram_recv.at[it, source],
            device_id={"cell": near(k)}, device_id_type=MESH,
        )

    def plane_copy(it, source, k):
        return pltpu.make_async_remote_copy(
            src_ref=planes.at[it, source], dst_ref=planes.at[it, source],
            send_sem=plane_send.at[it, k], recv_sem=plane_recv.at[it, source],
            device_id={"cell": far(k)}, device_id_type=MESH,
        )

    def total_copy(it):
        return pltpu.make_async_remote_copy(
            src_ref=totals.at[it], dst_ref=totals.at[it],
            send_sem=total_send.at[it], recv_sem=total_recv.at[it],
            device_id={"gene": other}, device_id_type=MESH,
        )

    def near_copy(it, group, source, k):
        return pltpu.make_async_remote_copy(
            src_ref=codes_out.at[it, group, lax.rem(spot + k, inner)],
            dst_ref=codes_in.at[it, group, source],
            send_sem=near_send.at[it, group, k], recv_sem=near_recv.at[it, group, source],
            device_id={"cell": near(k)}, device_id_type=MESH,
        )

    def step_copy(it, group, source, k):
        return pltpu.make_async_remote_copy(
            src_ref=steps_out.at[it, group, lax.rem(spot + k, inner)],
            dst_ref=steps_in.at[it, group, source],
            send_sem=step_send.at[it, group, k], recv_sem=step_recv.at[it, group, source],
            device_id={"cell": near(k)}, device_id_type=MESH,
        )

    def far_copy(it, source, k):
        return pltpu.make_async_remote_copy(
            src_ref=sums_own.at[it, lax.rem(here + k, outer)], dst_ref=sums_in.at[it, source],
            send_sem=far_send.at[it, k], recv_sem=far_recv.at[it, source],
            device_id={"cell": far(k)}, device_id_type=MESH,
        )

    def mid_copy(source, outward, along):
        target = lax.rem(here + outward, outer) * inner + lax.rem(spot + along, inner)
        return pltpu.make_async_remote_copy(
            src_ref=middle.at[source], dst_ref=middle.at[source],
            send_sem=mid_send.at[outward, along], recv_sem=mid_recv.at[source],
            device_id={"cell": target}, device_id_type=MESH,
        )

    def each_near(act):
        for k in range(1, inner):
            act(lax.rem(spot + inner - k, inner), k)

    def each_far(act):
        for k in range(1, outer):
            act(lax.rem(here + outer - k, outer), k)

    outwards = sorted(range(outer), key=lambda k: -min(k, outer - k))

    def each_mid(order, act):
        for outward in order:
            for along in range(inner):
                if outward + along > 0:
                    act(outward, along)

    def added(ref, count):
        total = ref[0]
        for c in range(1, count):
            total = total + ref[c]
        return total

    def loop(first, last, act):
        if last - first <= 4:
            for k in range(first, last):
                act(k)
        else:
            def body(k, _):
                act(k)
                return 0

            lax.fori_loop(first, last, body, 0)

    def part(r):
        return pl.ds(r * piece, piece)

    def place(r):
        for row in range(r * piece // side, (r + 1) * piece // side):
            for col in range(gene_blocks):
                dense[row * side : (row + 1) * side, col * side : (col + 1) * side] = held[
                    table[0, row * gene_blocks + col]
                ]

    def score(left, r, columns):
        return lax.dot_general(
            left, dense[part(r), columns], (((1,), (1,)), ((), ())),
            preferred_element_type=jnp.float32,
        )

    def iteration(it):
        if it == 0:
            with scope("place"):
                place(0)
            for r in range(parts):
                with scope("score"):
                    if r + 1 < parts:
                        place(r + 1)
                    mine[it, r] = score(first[...], r, slice(None))
                if r == 0:
                    with scope("barrier"):
                        pl.semaphore_wait(barrier, cells)
                pair_copy(it, r).start()
        else:
            order = outwards[::-1]
            for step, outward in enumerate(order):
                group = lax.rem(here + outward, outer)
                with scope("midwait"):
                    each_mid(
                        [outward],
                        lambda out, along: mid_copy(
                            group * inner + lax.rem(spot + along, inner), out, along
                        ).wait_recv(),
                    )
                left = jnp.concatenate(
                    [middle[group * inner + c] for c in range(inner)], axis=1
                )
                columns = pl.ds(pl.multiple_of(group * span, 128), span)
                with scope("score"):
                    for r in range(parts):
                        fresh = score(left, r, columns)
                        mine[it, r] = fresh if step == 0 else mine[it, r] + fresh
                        if step == outer - 1:
                            pair_copy(it, r).start()

        def merge(r):
            pair_copy(it, r).wait_recv()
            pieces = split_three(mine[it, r] + theirs[it, r])
            for i in range(it + 2):
                stacked[i * width : (i + 1) * width, part(r)] = pieces[i]

        with scope("merge"):
            for r in range(parts):
                merge(r)

        def product(columns):
            pair = jnp.dot(
                stacked[0 : 2 * width, :], columns, preferred_element_type=jnp.float32
            )
            return pair[:width] + pair[width:]

        def multiply(k):
            group = lax.rem(here + k, outer)
            wide = product(dense[:, pl.ds(pl.multiple_of(group * span, 128), span)])
            for c in range(inner):
                value = wide[:, c * chunk : (c + 1) * chunk]
                sums_near[group, c] = value
                coded, steps = encode(value)
                codes_out[it, group, c] = coded
                steps_out[it, group, c] = steps
            each_near(lambda _, k: near_copy(it, group, spot, k).start())
            each_near(lambda _, k: step_copy(it, group, spot, k).start())

        def gram():
            whole = stacked[0 : (it + 2) * width, :]
            cross = lax.dot_general(
                whole, whole, (((1,), (1,)), ((), ())), preferred_element_type=jnp.float32
            )
            cross = sum(cross[i * width : (i + 1) * width] for i in range(it + 2))
            total = sum(cross[:, i * width : (i + 1) * width] for i in range(it + 2))
            grams[it, spot] = jnp.concatenate([total[:half], total[half:]], axis=1)
            each_near(lambda _, k: gram_copy(it, spot, k).start())

        def forward(k):
            group = lax.rem(here + k, outer)
            each_near(lambda source, k: near_copy(it, group, source, k).wait_recv())
            each_near(lambda source, k: step_copy(it, group, source, k).wait_recv())
            total = sums_near[group, spot]
            for c in range(1, inner):
                source = lax.rem(spot + c, inner)
                total = total + decode(codes_in[it, group, source], steps_in[it, group, source])
            if isinstance(k, int) and k == 0:
                sums_in[it, here] = total
            else:
                sums_own[it, group] = total
                far_copy(it, here, k).start()

        with scope("gram"):
            pl.when(lead)(gram)
        with scope("multiply"):
            loop(1, outer + 1, multiply)

        @pl.when(lead)
        def _():
            with scope("gramwait"):
                each_near(lambda source, k: gram_copy(it, source, k).wait_recv())
            planes[it, here] = added(grams.at[it], inner)
            each_far(lambda _, k: plane_copy(it, here, k).start())

        with scope("forward"):
            loop(1, outer, forward)
            forward(0)

        @pl.when(lead)
        def _():
            with scope("planewait"):
                each_far(lambda source, k: plane_copy(it, source, k).wait_recv())
            totals[it] = added(planes.at[it], outer)
            total_copy(it).start()

        @pl.when(jnp.logical_not(lead))
        def _():
            with scope("totalwait"):
                total_copy(it).wait_recv()

        total = totals[it]
        total = jnp.concatenate([total[:, :width], total[:, width:]], axis=0)
        with scope("inverse"):
            inverse = inverse_factor(total)
        if it == 1:
            with scope("finish"):
                scale = jnp.sqrt(jnp.float32(cells * cell_dev))
                left = jnp.concatenate(
                    [jnp.concatenate([p] * 3, axis=1) for p in split_three(inverse)], axis=0
                )
                for r in range(parts):
                    final = jnp.dot(
                        left, stacked[:, part(r)], preferred_element_type=jnp.float32
                    )
                    final = final[:width] + final[width : 2 * width] + final[2 * width :]
                    basis_out[:, part(r)] = (final * scale).astype(basis_out.dtype)
        with scope("farwait"):
            each_far(lambda source, k: far_copy(it, source, k).wait_recv())
        with scope("result"):
            summed = added(sums_in.at[it], outer)
            result = jnp.dot(inverse, summed, precision=HIGH, preferred_element_type=jnp.float32)
            if it == 0:
                middle[cell] = result.astype(middle.dtype)
                each_mid(outwards, lambda out, along: mid_copy(cell, out, along).start())
            else:
                load_out[...] = result

    iteration(0)
    iteration(1)

    for it in range(2):
        for r in range(parts):
            pair_copy(it, r).wait_send()

        @pl.when(lead)
        def _():
            each_near(lambda _, k: gram_copy(it, spot, k).wait_send())
            each_far(lambda _, k: plane_copy(it, here, k).wait_send())
            total_copy(it).wait_send()

        loop(0, outer, lambda group: each_near(
            lambda _, k: near_copy(it, group, spot, k).wait_send()
        ))
        loop(0, outer, lambda group: each_near(
            lambda _, k: step_copy(it, group, spot, k).wait_send()
        ))
        each_far(lambda _, k: far_copy(it, here, k).wait_send())
    each_mid(outwards, lambda out, along: mid_copy(cell, out, along).wait_send())


def local(cells, genes, tiles, tile_row, tile_col, tile_count, start_basis):
    slots, side = tiles.shape[1], tiles.shape[-1]
    width, gene_dev = start_basis.shape
    gene_blocks = gene_dev // side
    cell_dev = ROW_BLOCKS * side
    chunk = gene_dev // cells
    parts = 2
    inner = 1
    while inner * inner * 4 <= cells and cells % (inner * 2) == 0:
        inner = inner * 2
    outer = cells // inner
    places = ROW_BLOCKS * gene_blocks
    dma = pltpu.SemaphoreType.DMA
    return pl.pallas_call(
        functools.partial(kernel, cells, inner, genes, parts),
        out_shape=(
            jax.ShapeDtypeStruct((width, cell_dev), jnp.bfloat16),
            jax.ShapeDtypeStruct((width, chunk), jnp.float32),
        ),
        in_specs=[
            pl.BlockSpec(memory_space=pltpu.SMEM),
            pl.BlockSpec(memory_space=pltpu.HBM),
            pl.BlockSpec(memory_space=pltpu.HBM),
            pl.BlockSpec(memory_space=pltpu.HBM),
            pl.BlockSpec(memory_space=pltpu.HBM),
        ],
        out_specs=(
            pl.BlockSpec(memory_space=pltpu.VMEM),
            pl.BlockSpec(memory_space=pltpu.VMEM),
        ),
        scratch_shapes=[
            pltpu.VMEM((1, slots), jnp.int32),
            pltpu.VMEM((1, slots), jnp.int32),
            pltpu.VMEM((1, places), jnp.int32),
            pltpu.SMEM((1, places), jnp.int32),
            pltpu.VMEM((slots + 1, side, side), jnp.bfloat16),
            pltpu.VMEM((cell_dev, gene_dev), jnp.bfloat16),
            pltpu.VMEM((width, gene_dev), jnp.bfloat16),
            pltpu.VMEM((2, parts, width, cell_dev // parts), jnp.float32),
            pltpu.VMEM((2, parts, width, cell_dev // parts), jnp.float32),
            pltpu.VMEM((3 * width, cell_dev), jnp.bfloat16),
            pltpu.VMEM((2, inner, width // 2, 2 * width), jnp.float32),
            pltpu.VMEM((2, outer, width // 2, 2 * width), jnp.float32),
            pltpu.VMEM((2, width // 2, 2 * width), jnp.float32),
            pltpu.VMEM((outer, inner, width, chunk), jnp.float32),
            pltpu.VMEM((2, outer, inner, width, chunk), jnp.int16),
            pltpu.VMEM((2, outer, inner, width, chunk), jnp.int16),
            pltpu.VMEM((2, outer, inner, 1, width), jnp.float32),
            pltpu.VMEM((2, outer, inner, 1, width), jnp.float32),
            pltpu.VMEM((2, outer, width, chunk), jnp.float32),
            pltpu.VMEM((2, outer, width, chunk), jnp.float32),
            pltpu.VMEM((cells, width, chunk), jnp.bfloat16),
            dma, dma((2,)), dma, dma,
            dma((2, parts)), dma((2, parts)),
            dma((2, inner)), dma((2, inner)), dma((2, outer)), dma((2, outer)), dma((2,)), dma((2,)),
            dma((2, outer, inner)), dma((2, outer, inner)),
            dma((2, outer, inner)), dma((2, outer, inner)), dma((2, outer)), dma((2, outer)),
            dma((outer, inner)), dma((cells,)),
        ],
        compiler_params=pltpu.CompilerParams(
            collective_id=0, has_side_effects=True, vmem_limit_bytes=36 * 1024 * 1024
        ),
    )(tile_count, *(
        pltpu.with_memory_space_constraint(array, pltpu.HBM)
        for array in (tile_row, tile_col, tiles[0], start_basis)
    ))


def solution(mesh):
    return jax.shard_map(
        functools.partial(local, mesh.shape["cell"], mesh.shape["gene"]),
        mesh=mesh,
        in_specs=(
            P("gene", "cell", None, None),
            P("gene", "cell"),
            P("gene", "cell"),
            P("gene", "cell"),
            P(None, "gene"),
        ),
        out_specs=(P(None, "cell"), P(None, ("gene", "cell"))),
        check_vma=False,
    )
```

time: 48.5 us -> 43.3 us (0.89)
  Pallas kernels: 45.8 us -> 40.5 us
    pallas_call x1, Pallas kernels: 45.8 us -> 40.5 us  [local(): pl.pallas_call(functools.partial(kernel, cells, inner, genes, parts), out...]
where the time goes in v2:
time: 43.3 us; the launch traced here: 43.1 us
  Pallas kernels  40.5 us (94%)
  between operations  1.29 us (3%)
  local copies, waits for them, and re-layouts  1.27 us (3%)
    pallas_call x1, Pallas kernels, local(): pl.pallas_call(functools.partial(kernel, cells, inner, genes, parts), out...  40.5 us
    unnamed x2, local copies, waits for them, and re-layouts  1.27 us

profile of v2, /device:TPU:0, one launch (start us, length us, event | category | flops | bytes accessed | tf_op | source)
XLA Modules:
  0.0 43.1 jit_solution(1244835900659955965)
XLA Ops:
  1.3 40.5 %shard_map.68 = (bf16[64,1024]{1,0:T(8,128)(2,1)S(1)}, f32[64,128]{1,0:T(8,128)S(1)}) custom-call(s32[1,1]{1,0:T(1,128)S(6)} %copy.9.slot_count, s32[1,64]{1,0:T(1,128)} %slot_row.1, s32[1,64]{1,0:T(1,128)} %slot_col.1, bf16[64,128,128]{2,1,0:T(8,128)(2,1)} %bitcast.1, bf16[64,2048]{1,0:T(8,128)(2,1)} %start.1), custom_call_target="tpu_custom_call" | custom-call | tf_op jit(solution)/shard_map/pallas_call | solution.py:451
  41.8 0.7 %copy.10 = bf16[64,1024]{1,0:T(8,128)(2,1)} copy(bf16[64,1024]{1,0:T(8,128)(2,1)S(1)} %get-tuple-element.4) | data formatting | bytes 262144
  42.5 0.6 %copy.11 = f32[64,128]{1,0:T(8,128)} copy(f32[64,128]{1,0:T(8,128)S(1)} %get-tuple-element.5) | data formatting | bytes 65536

commit v3 on v2

v3 whole, which is shorter than its diff:
```python
import functools

import jax
import jax.numpy as jnp
from jax import lax
from jax.experimental import pallas as pl
from jax.experimental.pallas import tpu as pltpu
from jax.sharding import PartitionSpec as P

ROW_BLOCKS = 8
PANEL = 4
LEVELS = 32766.0
MESH = pl.DeviceIdType.MESH
HIGH = lax.Precision.HIGHEST
scope = jax.named_scope


def split_three(value):
    high = value.astype(jnp.bfloat16)
    rest = value - high.astype(jnp.float32)
    middle = rest.astype(jnp.bfloat16)
    low = (rest - middle.astype(jnp.float32)).astype(jnp.bfloat16)
    return high, middle, low


def inverse_factor(gram):
    width = gram.shape[0]
    shape = (width, 2 * width)
    row = lax.broadcasted_iota(jnp.int32, shape, 0)
    lane = lax.broadcasted_iota(jnp.int32, shape, 1)
    both = jnp.concatenate([jnp.zeros_like(gram), gram], axis=1)
    both = jnp.where(row == lane, 1.0, both)
    pivots = jnp.ones(shape, jnp.float32)
    done = []
    start = 0

    def spread(first):
        return {
            j: jnp.broadcast_to(both[:, width + j : width + j + 1], both.shape)
            for j in range(first, min(first + PANEL, width))
        }

    ahead = spread(0)
    for first in range(0, width, PANEL):
        base = first // 8 * 8
        if base > start:
            done.append((both[: base - start], pivots[: base - start]))
            both = both[base - start :]
            pivots = pivots[base - start :]
            row = row[base - start :]
            ahead = {j: column[base - start :] for j, column in ahead.items()}
            start = base
        columns = ahead
        ahead = spread(first + PANEL)
        for j in range(first, first + PANEL):
            at = j - start
            column = columns.pop(j)
            pivot = column[at : at + 1]
            factor = jnp.where(row > j, column * (1.0 / pivot), 0.0)
            pivots = jnp.where(row == j, pivot, pivots)
            both = both - factor * both[at : at + 1]
            for later in (columns, ahead):
                for m in later:
                    later[m] = later[m] - factor * later[m][at : at + 1]
    done.append((both, pivots))
    both = jnp.concatenate([piece for piece, _ in done], axis=0)
    pivots = jnp.concatenate([piece for _, piece in done], axis=0)
    return (both * lax.rsqrt(pivots))[:, :width]


def diagonal(width):
    square = (width, width)
    return lax.broadcasted_iota(jnp.int32, square, 0) == lax.broadcasted_iota(jnp.int32, square, 1)


def encode(value):
    peak = jnp.max(jnp.abs(value), axis=1, keepdims=True)
    step = jnp.maximum(peak, 1e-30) * (1.0 / LEVELS)
    coded = jnp.round(value * (1.0 / step)).astype(jnp.int32).astype(jnp.int16)
    square = (value.shape[0], value.shape[0])
    turned = jnp.where(diagonal(square[0]), jnp.broadcast_to(step, square), 0.0)
    return coded, jnp.sum(turned, axis=0, keepdims=True)


def decode(coded, steps):
    square = (coded.shape[0], coded.shape[0])
    turned = jnp.where(diagonal(square[0]), jnp.broadcast_to(steps, square), 0.0)
    step = jnp.sum(turned, axis=1, keepdims=True)
    return coded.astype(jnp.int32).astype(jnp.float32) * step


def kernel(
    cells, inner, genes, parts,
    slot_count, slot_row, slot_col, tiles, start, basis_out, load_out,
    slots_in, places_out, table, held, dense, first, mine, theirs, stacked, grams, planes, factor,
    sums_near, codes_out, codes_in, steps_out, steps_in, sums_own, sums_in,
    columns, middle, load_res, load_in,
    tile_sem, slot_sem, table_sem, start_sem, pair_send, pair_recv,
    gram_send, gram_recv, plane_send, plane_recv, factor_send, factor_recv,
    near_send, near_recv, step_send, step_recv, far_send, far_recv,
    column_send, column_recv, mid_send, mid_recv, load_send, load_recv,
):
    cell = lax.axis_index("cell")
    gene = lax.axis_index("gene")
    slots, side, _ = tiles.shape
    width = start.shape[0]
    cell_dev, gene_dev = dense.shape
    gene_blocks = gene_dev // side
    chunk = gene_dev // cells
    piece = cell_dev // parts
    half = width // 2
    outer = cells // inner
    span = inner * chunk
    here = cell // inner
    spot = lax.rem(cell, inner)
    other = lax.rem(gene + 1, genes)
    head = genes - 1
    lead = gene == head
    follow = gene != head

    slot_copies = [
        pltpu.make_async_copy(slot_row, slots_in.at[0], slot_sem.at[0]),
        pltpu.make_async_copy(slot_col, slots_in.at[1], slot_sem.at[1]),
    ]
    for copy in slot_copies:
        copy.start()
    fetch = pltpu.make_async_copy(tiles, held.at[pl.ds(0, slots)], tile_sem)
    fetch.start()
    first_basis = pltpu.make_async_copy(start, first, start_sem)
    first_basis.start()

    def near(k):
        return here * inner + lax.rem(spot + k, inner)

    def far(k):
        return lax.rem(here + k, outer) * inner + spot

    barrier = pltpu.get_barrier_semaphore()
    greeted = 0
    for k in range(inner):
        for g in range(genes):
            if k + g > 0:
                pl.semaphore_signal(
                    barrier, inc=1,
                    device_id={"cell": near(k), "gene": lax.rem(gene + g, genes)},
                    device_id_type=MESH,
                )
                greeted += 1
    for k in range(1, outer):
        pl.semaphore_signal(barrier, inc=1, device_id={"cell": far(k)}, device_id_type=MESH)
        greeted += 1

    held[slots] = jnp.zeros((side, side), held.dtype)
    for copy in slot_copies:
        copy.wait()
    places = (cell_dev // side) * gene_blocks
    lane = lax.broadcasted_iota(jnp.int32, (1, slots), 1)
    spots = jnp.where(
        lane < slot_count[0, 0], slots_in[0] * gene_blocks + slots_in[1], places
    )
    square = (slots, slots)
    turned = jnp.where(diagonal(slots), jnp.broadcast_to(spots, square), 0)
    turned = jnp.sum(turned, axis=1, keepdims=True)
    flat = (slots, places)
    found = jnp.broadcast_to(turned, flat) == lax.broadcasted_iota(jnp.int32, flat, 1)
    found = jnp.where(found, lax.broadcasted_iota(jnp.int32, flat, 0), slots)
    places_out[...] = jnp.min(found, axis=0, keepdims=True)
    listing = pltpu.make_async_copy(places_out, table, table_sem)
    listing.start()
    listing.wait()
    fetch.wait()
    first_basis.wait()

    def remote(source, target, send_sem, recv_sem, **device):
        return pltpu.make_async_remote_copy(
            src_ref=source, dst_ref=target, send_sem=send_sem, recv_sem=recv_sem,
            device_id=device, device_id_type=MESH,
        )

    def pair_copy(it, r):
        return remote(
            mine.at[it, r], theirs.at[it, r], pair_send.at[0], pair_recv.at[it, r], gene=other
        )

    def gram_copy(it, k):
        return remote(
            grams.at[it, spot], grams.at[it, spot], gram_send.at[0], gram_recv.at[it],
            cell=near(k),
        )

    def plane_copy(it, k):
        return remote(
            planes.at[it, here], planes.at[it, here], plane_send.at[0], plane_recv.at[it],
            cell=far(k),
        )

    def near_copy(it, group, k):
        return remote(
            codes_out.at[it, group, k], codes_in.at[it, gene, group, k],
            near_send.at[0], near_recv.at[it, gene, group], cell=near(k), gene=head,
        )

    def step_copy(it, group, k):
        return remote(
            steps_out.at[it, group, k], steps_in.at[it, gene, group, k],
            step_send.at[0], step_recv.at[it, gene, group], cell=near(k), gene=head,
        )

    def far_copy(it, k):
        return remote(
            sums_own.at[it, lax.rem(here + k, outer)], sums_in.at[it, here],
            far_send.at[0], far_recv.at[it], cell=far(k),
        )

    def column_copy(target):
        return remote(
            columns.at[here], columns.at[here], column_send.at[0], column_recv.at[here],
            cell=target * inner + spot,
        )

    def mid_copy(group, g, k):
        return remote(
            columns.at[group, g], middle.at[group * inner + spot],
            mid_send.at[group], mid_recv.at[group], cell=near(k), gene=g,
        )

    def awaited(refs, sem):
        remote(refs, refs, pair_send.at[0], sem, gene=other).wait_recv()

    def drained(refs, sem):
        remote(refs, refs, sem, pair_recv.at[0, 0], gene=other).wait_send()

    def added(ref, count):
        total = ref[0]
        for c in range(1, count):
            total = total + ref[c]
        return total

    def loop(first, last, act):
        if last - first <= 4:
            for k in range(first, last):
                act(k)
        else:
            def body(k, _):
                act(k)
                return 0

            lax.fori_loop(first, last, body, 0)

    def part(r):
        return pl.ds(r * piece, piece)

    def along(m):
        return lax.rem(here + jnp.where(2 * here < outer, m, outer - m), outer)

    def place(r):
        for row in range(r * piece // side, (r + 1) * piece // side):
            for col in range(gene_blocks):
                dense[row * side : (row + 1) * side, col * side : (col + 1) * side] = held[
                    table[0, row * gene_blocks + col]
                ]

    def score(left, r, lanes):
        return lax.dot_general(
            left, dense[part(r), lanes], (((1,), (1,)), ((), ())),
            preferred_element_type=jnp.float32,
        )

    def first_scores():
        with scope("place"):
            place(0)
        for r in range(parts):
            with scope("score"):
                if r + 1 < parts:
                    place(r + 1)
                mine[0, r] = score(first[...], r, slice(None))
            if r == 0:
                with scope("barrier"):
                    pl.semaphore_wait(barrier, greeted)
            pair_copy(0, r).start()

    def second_scores():
        def step(m):
            group = along(m)
            with scope("midwait"):
                @pl.when(lead)
                def _():
                    awaited(middle.at[pl.ds(0, inner - 1)], mid_recv.at[group])
                    middle[group * inner + spot] = columns[group, head]

                @pl.when(follow)
                def _():
                    awaited(middle.at[pl.ds(0, inner)], mid_recv.at[group])

            left = jnp.concatenate([middle[group * inner + c] for c in range(inner)], axis=1)
            lanes = pl.ds(pl.multiple_of(group * span, 128), span)
            with scope("score"):
                for r in range(parts):
                    fresh = score(left, r, lanes)
                    if isinstance(m, int) and m == 0:
                        mine[1, r] = fresh
                    else:
                        mine[1, r] = mine[1, r] + fresh
                    if isinstance(m, int) and m == outer - 1:
                        pair_copy(1, r).start()

        step(0)
        loop(1, outer - 1, step)
        step(outer - 1)

    def share(group):
        for k in list(range(1, inner)) + [0]:
            for g in range(genes):
                if k > 0 or g != head:
                    mid_copy(group, g, k).start()

    def iteration(it):
        if it == 0:
            first_scores()
        else:
            second_scores()

        with scope("merge"):
            for r in range(parts):
                pair_copy(it, r).wait_recv()
                pieces = split_three(mine[it, r] + theirs[it, r])
                for i in range(it + 2):
                    stacked[i * width : (i + 1) * width, part(r)] = pieces[i]

        def gram():
            whole = stacked[0 : (it + 2) * width, :]
            cross = lax.dot_general(
                whole, whole, (((1,), (1,)), ((), ())), preferred_element_type=jnp.float32
            )
            cross = sum(cross[i * width : (i + 1) * width] for i in range(it + 2))
            total = sum(cross[:, i * width : (i + 1) * width] for i in range(it + 2))
            grams[it, spot] = jnp.concatenate([total[:half], total[half:]], axis=1)
            for k in range(1, inner):
                gram_copy(it, k).start()

        def multiply(m):
            group = lax.rem(here + m, outer)
            wide = jnp.dot(
                stacked[0 : 2 * width, :],
                dense[:, pl.ds(pl.multiple_of(group * span, 128), span)],
                preferred_element_type=jnp.float32,
            )
            wide = wide[:width] + wide[width:]
            for c in range(inner):
                sums_near[group, c] = wide[:, c * chunk : (c + 1) * chunk]
            for k in range(inner):
                coded, steps = encode(sums_near[group, lax.rem(spot + k, inner)])
                codes_out[it, group, k] = coded
                steps_out[it, group, k] = steps
            for k in range(1, inner):
                step_copy(it, group, k).start()
                near_copy(it, group, k).start()

            @pl.when(follow)
            def _():
                step_copy(it, group, 0).start()
                near_copy(it, group, 0).start()

        def forward(m):
            group = lax.rem(here + m, outer)
            own = isinstance(m, int) and m == 0
            for g in range(genes):
                low = 1 if g == head else 0
                awaited(steps_in.at[it, g, group, pl.ds(low, inner - low)], step_recv.at[it, g, group])
                awaited(codes_in.at[it, g, group, pl.ds(low, inner - low)], near_recv.at[it, g, group])
                total = sums_near[group, spot] if g == head else None
                for k in range(low, inner):
                    value = decode(codes_in[it, g, group, k], steps_in[it, g, group, k])
                    total = value if total is None else total + value
                if own:
                    sums_in[it, here, g] = total
                else:
                    sums_own[it, group, g] = total
            if not own:
                far_copy(it, m).start()

        def reduce():
            with scope("gramwait"):
                awaited(grams.at[it, pl.ds(0, inner - 1)], gram_recv.at[it])
            planes[it, here] = added(grams.at[it], inner)
            for k in range(1, outer):
                plane_copy(it, k).start()
            with scope("forward"):
                loop(1, outer, forward)
                forward(0)
            with scope("planewait"):
                awaited(planes.at[it, pl.ds(0, outer - 1)], plane_recv.at[it])
            total = added(planes.at[it], outer)
            total = jnp.concatenate([total[:, :width], total[:, width:]], axis=0)
            with scope("inverse"):
                inverse = inverse_factor(total)
            if it == 1:
                factor[...] = inverse
                remote(factor, factor, factor_send.at[0], factor_recv.at[0], gene=other).start()
            with scope("farwait"):
                awaited(sums_in.at[it, pl.ds(0, outer - 1)], far_recv.at[it])
            with scope("result"):
                summed = added(sums_in.at[it], outer)
                summed = jnp.concatenate([summed[g] for g in range(genes)], axis=1)
                result = jnp.dot(
                    inverse, summed, precision=HIGH, preferred_element_type=jnp.float32
                )
                result = [result[:, g * chunk : (g + 1) * chunk] for g in range(genes)]
                if it == 0:
                    for g in range(genes):
                        columns[here, g] = result[g].astype(columns.dtype)
                    for m in range(outer - 1, 0, -1):
                        column_copy(along(m)).start()
                    share(here)
                else:
                    load_res[...] = result[0]
                    remote(load_res, load_in, load_send.at[0], load_recv.at[0], gene=other).start()
                    load_out[...] = result[head]
            if it == 0:
                def relay(m):
                    group = along(m)
                    with scope("columnwait"):
                        awaited(columns.at[group], column_recv.at[group])
                    share(group)

                loop(1, outer, relay)

        with scope("gram"):
            pl.when(lead)(gram)
        with scope("multiply"):
            loop(1, outer + 1, multiply)
        pl.when(lead)(reduce)

    iteration(0)
    iteration(1)

    @pl.when(follow)
    def _():
        with scope("factorwait"):
            awaited(factor, factor_recv.at[0])

    with scope("finish"):
        scale = jnp.sqrt(jnp.float32(cells * cell_dev))
        left = jnp.concatenate(
            [jnp.concatenate([p] * 3, axis=1) for p in split_three(factor[...])], axis=0
        )
        for r in range(parts):
            final = jnp.dot(left, stacked[:, part(r)], preferred_element_type=jnp.float32)
            final = final[:width] + final[width : 2 * width] + final[2 * width :]
            basis_out[:, part(r)] = (final * scale).astype(basis_out.dtype)

    @pl.when(follow)
    def _():
        with scope("loadwait"):
            awaited(load_in, load_recv.at[0])
        load_out[...] = load_in[...]
        drained(codes_out, near_send.at[0])
        drained(steps_out, step_send.at[0])

    @pl.when(lead)
    def _():
        drained(codes_out.at[:, :, pl.ds(1, inner - 1)], near_send.at[0])
        drained(steps_out.at[:, :, pl.ds(1, inner - 1)], step_send.at[0])
        drained(grams.at[:, pl.ds(0, inner - 1)], gram_send.at[0])
        drained(planes.at[:, pl.ds(0, outer - 1)], plane_send.at[0])
        drained(sums_own.at[:, pl.ds(0, outer - 1)], far_send.at[0])
        drained(columns.at[pl.ds(0, outer - 1)], column_send.at[0])
        loop(0, outer, lambda group: drained(
            middle.at[pl.ds(0, inner * genes - 1)], mid_send.at[group]
        ))
        drained(factor, factor_send.at[0])
        drained(load_res, load_send.at[0])

    drained(mine, pair_send.at[0])


def local(cells, genes, tiles, tile_row, tile_col, tile_count, start_basis):
    slots, side = tiles.shape[1], tiles.shape[-1]
    width, gene_dev = start_basis.shape
    gene_blocks = gene_dev // side
    cell_dev = ROW_BLOCKS * side
    chunk = gene_dev // cells
    parts = 2
    inner = 1
    while inner * inner * 4 <= cells and cells % (inner * 2) == 0:
        inner = inner * 2
    outer = cells // inner
    places = ROW_BLOCKS * gene_blocks
    dma = pltpu.SemaphoreType.DMA
    return pl.pallas_call(
        functools.partial(kernel, cells, inner, genes, parts),
        out_shape=(
            jax.ShapeDtypeStruct((width, cell_dev), jnp.bfloat16),
            jax.ShapeDtypeStruct((width, chunk), jnp.float32),
        ),
        in_specs=[
            pl.BlockSpec(memory_space=pltpu.SMEM),
            pl.BlockSpec(memory_space=pltpu.HBM),
            pl.BlockSpec(memory_space=pltpu.HBM),
            pl.BlockSpec(memory_space=pltpu.HBM),
            pl.BlockSpec(memory_space=pltpu.HBM),
        ],
        out_specs=(
            pl.BlockSpec(memory_space=pltpu.VMEM),
            pl.BlockSpec(memory_space=pltpu.VMEM),
        ),
        scratch_shapes=[
            pltpu.VMEM((2, 1, slots), jnp.int32),
            pltpu.VMEM((1, places), jnp.int32),
            pltpu.SMEM((1, places), jnp.int32),
            pltpu.VMEM((slots + 1, side, side), jnp.bfloat16),
            pltpu.VMEM((cell_dev, gene_dev), jnp.bfloat16),
            pltpu.VMEM((width, gene_dev), jnp.bfloat16),
            pltpu.VMEM((2, parts, width, cell_dev // parts), jnp.float32),
            pltpu.VMEM((2, parts, width, cell_dev // parts), jnp.float32),
            pltpu.VMEM((3 * width, cell_dev), jnp.bfloat16),
            pltpu.VMEM((2, inner, width // 2, 2 * width), jnp.float32),
            pltpu.VMEM((2, outer, width // 2, 2 * width), jnp.float32),
            pltpu.VMEM((width, width), jnp.float32),
            pltpu.VMEM((outer, inner, width, chunk), jnp.float32),
            pltpu.VMEM((2, outer, inner, width, chunk), jnp.int16),
            pltpu.VMEM((2, genes, outer, inner, width, chunk), jnp.int16),
            pltpu.VMEM((2, outer, inner, 1, width), jnp.float32),
            pltpu.VMEM((2, genes, outer, inner, 1, width), jnp.float32),
            pltpu.VMEM((2, outer, genes, width, chunk), jnp.float32),
            pltpu.VMEM((2, outer, genes, width, chunk), jnp.float32),
            pltpu.VMEM((outer, genes, width, chunk), jnp.bfloat16),
            pltpu.VMEM((cells, width, chunk), jnp.bfloat16),
            pltpu.VMEM((width, chunk), jnp.float32),
            pltpu.VMEM((width, chunk), jnp.float32),
            dma, dma((2,)), dma, dma,
            dma((1,)), dma((2, parts)),
            dma((1,)), dma((2,)), dma((1,)), dma((2,)), dma((1,)), dma((1,)),
            dma((1,)), dma((2, genes, outer)), dma((1,)), dma((2, genes, outer)),
            dma((1,)), dma((2,)),
            dma((1,)), dma((outer,)), dma((outer,)), dma((outer,)), dma((1,)), dma((1,)),
        ],
        compiler_params=pltpu.CompilerParams(
            collective_id=0, has_side_effects=True, vmem_limit_bytes=44 * 1024 * 1024
        ),
    )(tile_count, *(
        pltpu.with_memory_space_constraint(array, pltpu.HBM)
        for array in (tile_row, tile_col, tiles[0], start_basis)
    ))


def solution(mesh):
    return jax.shard_map(
        functools.partial(local, mesh.shape["cell"], mesh.shape["gene"]),
        mesh=mesh,
        in_specs=(
            P("gene", "cell", None, None),
            P("gene", "cell"),
            P("gene", "cell"),
            P("gene", "cell"),
            P(None, "gene"),
        ),
        out_specs=(P(None, "cell"), P(None, ("gene", "cell"))),
        check_vma=False,
    )
```

time: 43.3 us -> 38.9 us (0.90)
  Pallas kernels: 40.5 us -> 36.1 us
    pallas_call x1, Pallas kernels: 40.5 us -> 36.1 us  [local(): pl.pallas_call(functools.partial(kernel, cells, inner, genes, parts), out...]
where the time goes in v3:
time: 38.9 us; the launch traced here: 38.7 us
  Pallas kernels  36.1 us (93%)
  between operations  1.29 us (3%)
  local copies, waits for them, and re-layouts  1.27 us (3%)
    pallas_call x1, Pallas kernels, local(): pl.pallas_call(functools.partial(kernel, cells, inner, genes, parts), out...  36.1 us
    unnamed x2, local copies, waits for them, and re-layouts  1.27 us

profile of v3, /device:TPU:0, one launch (start us, length us, event | category | flops | bytes accessed | tf_op | source)
XLA Modules:
  0.0 38.7 jit_solution(7760777877210218175)
XLA Ops:
  1.3 36.1 %shard_map.68 = (bf16[64,1024]{1,0:T(8,128)(2,1)S(1)}, f32[64,128]{1,0:T(8,128)S(1)}) custom-call(s32[1,1]{1,0:T(1,128)S(6)} %copy.9.slot_count, s32[1,64]{1,0:T(1,128)} %slot_row.1, s32[1,64]{1,0:T(1,128)} %slot_col.1, bf16[64,128,128]{2,1,0:T(8,128)(2,1)} %bitcast.1, bf16[64,2048]{1,0:T(8,128)(2,1)} %start.1), custom_call_target="tpu_custom_call" | custom-call | tf_op jit(solution)/shard_map/pallas_call | solution.py:490
  37.4 0.7 %copy.10 = bf16[64,1024]{1,0:T(8,128)(2,1)} copy(bf16[64,1024]{1,0:T(8,128)(2,1)S(1)} %get-tuple-element.4) | data formatting | bytes 262144
  38.1 0.6 %copy.11 = f32[64,128]{1,0:T(8,128)} copy(f32[64,128]{1,0:T(8,128)S(1)} %get-tuple-element.5) | data formatting | bytes 65536

commit v4 on v3

--- a/solution.py
+++ b/solution.py
@@ -73,19 +73,25 @@
     return lax.broadcasted_iota(jnp.int32, square, 0) == lax.broadcasted_iota(jnp.int32, square, 1)
 
 
+def turn(column):
+    square = (column.shape[0], column.shape[0])
+    turned = jnp.where(diagonal(square[0]), jnp.broadcast_to(column, square), 0.0)
+    return jnp.sum(turned, axis=0, keepdims=True)
+
+
+def turn_back(line, lanes):
+    square = (line.shape[1], line.shape[1])
+    turned = jnp.where(diagonal(square[0]), jnp.broadcast_to(line, square), 0.0)
+    return jnp.broadcast_to(jnp.sum(turned, axis=1, keepdims=True), (square[0], lanes))
+
+
 def encode(value):
-    peak = jnp.max(jnp.abs(value), axis=1, keepdims=True)
+    peak = jnp.max(jnp.abs(value), axis=0, keepdims=True)
     step = jnp.maximum(peak, 1e-30) * (1.0 / LEVELS)
-    coded = jnp.round(value * (1.0 / step)).astype(jnp.int32).astype(jnp.int16)
-    square = (value.shape[0], value.shape[0])
-    turned = jnp.where(diagonal(square[0]), jnp.broadcast_to(step, square), 0.0)
-    return coded, jnp.sum(turned, axis=0, keepdims=True)
-
-
-def decode(coded, steps):
-    square = (coded.shape[0], coded.shape[0])
-    turned = jnp.where(diagonal(square[0]), jnp.broadcast_to(steps, square), 0.0)
-    step = jnp.sum(turned, axis=1, keepdims=True)
+    return jnp.round(value * (1.0 / step)).astype(jnp.int32).astype(jnp.int16), step
+
+
+def decode(coded, step):
     return coded.astype(jnp.int32).astype(jnp.float32) * step
 
 
@@ -93,11 +99,12 @@
     cells, inner, genes, parts,
     slot_count, slot_row, slot_col, tiles, start, basis_out, load_out,
     slots_in, places_out, table, held, dense, first, mine, theirs, stacked, grams, planes, factor,
-    sums_near, codes_out, codes_in, steps_out, steps_in, sums_own, sums_in,
+    sums_near, codes_out, codes_in, steps_out, steps_in, lines_out, lines_in, factors,
+    sums_own, sums_in,
     columns, middle, load_res, load_in,
     tile_sem, slot_sem, table_sem, start_sem, pair_send, pair_recv,
     gram_send, gram_recv, plane_send, plane_recv, factor_send, factor_recv,
-    near_send, near_recv, step_send, step_recv, far_send, far_recv,
+    near_send, near_recv, step_send, step_recv, line_send, line_recv, far_send, far_recv,
     column_send, column_recv, mid_send, mid_recv, load_send, load_recv,
 ):
     cell = lax.axis_index("cell")
@@ -206,10 +213,16 @@
             step_send.at[0], step_recv.at[it, gene, group], cell=near(k), gene=head,
         )
 
-    def far_copy(it, k):
-        return remote(
-            sums_own.at[it, lax.rem(here + k, outer)], sums_in.at[it, here],
-            far_send.at[0], far_recv.at[it], cell=far(k),
+    def line_copy(it, k):
+        return remote(
+            lines_out.at[it], lines_in.at[it, gene, k],
+            line_send.at[0], line_recv.at[it, gene], cell=near(k), gene=head,
+        )
+
+    def far_copy(it, group):
+        return remote(
+            sums_own.at[it, group], sums_in.at[it, here],
+            far_send.at[0], far_recv.at[it], cell=group * inner + spot,
         )
 
     def column_copy(target):
@@ -253,9 +266,9 @@
     def along(m):
         return lax.rem(here + jnp.where(2 * here < outer, m, outer - m), outer)
 
-    def place(r):
-        for row in range(r * piece // side, (r + 1) * piece // side):
-            for col in range(gene_blocks):
+    def place(low, high):
+        for row in range(cell_dev // side):
+            for col in range(low, high):
                 dense[row * side : (row + 1) * side, col * side : (col + 1) * side] = held[
                     table[0, row * gene_blocks + col]
                 ]
@@ -267,17 +280,22 @@
         )
 
     def first_scores():
+        stages = 4
+        share_cols = gene_blocks // stages
         with scope("place"):
-            place(0)
-        for r in range(parts):
+            place(0, share_cols)
+        for q in range(stages):
+            lanes = slice(q * share_cols * side, (q + 1) * share_cols * side)
             with scope("score"):
-                if r + 1 < parts:
-                    place(r + 1)
-                mine[0, r] = score(first[...], r, slice(None))
-            if r == 0:
-                with scope("barrier"):
-                    pl.semaphore_wait(barrier, greeted)
-            pair_copy(0, r).start()
+                if q + 1 < stages:
+                    place((q + 1) * share_cols, (q + 2) * share_cols)
+                for r in range(parts):
+                    fresh = score(first[:, lanes], r, lanes)
+                    mine[0, r] = fresh if q == 0 else mine[0, r] + fresh
+                    if q == stages - 1:
+                        if r == 0:
+                            pl.semaphore_wait(barrier, greeted)
+                        pair_copy(0, r).start()
 
     def second_scores():
         def step(m):
@@ -321,11 +339,25 @@
             second_scores()
 
         with scope("merge"):
+            peak = None
             for r in range(parts):
                 pair_copy(it, r).wait_recv()
-                pieces = split_three(mine[it, r] + theirs[it, r])
+                whole = mine[it, r] + theirs[it, r]
+                most = jnp.max(jnp.abs(whole), axis=1, keepdims=True)
+                peak = most if peak is None else jnp.maximum(peak, most)
+                pieces = split_three(whole)
                 for i in range(it + 2):
                     stacked[i * width : (i + 1) * width, part(r)] = pieces[i]
+
+            peak = jnp.maximum(peak, 1e-30)
+            lines_out[it] = turn(peak)
+            shrink = jnp.broadcast_to(1.0 / peak, (width, chunk))
+            for k in range(1, inner):
+                line_copy(it, k).start()
+
+            @pl.when(follow)
+            def _():
+                line_copy(it, 0).start()
 
         def gram():
             whole = stacked[0 : (it + 2) * width, :]
@@ -339,7 +371,7 @@
                 gram_copy(it, k).start()
 
         def multiply(m):
-            group = lax.rem(here + m, outer)
+            group = along(outer - m)
             wide = jnp.dot(
                 stacked[0 : 2 * width, :],
                 dense[:, pl.ds(pl.multiple_of(group * span, 128), span)],
@@ -349,7 +381,7 @@
             for c in range(inner):
                 sums_near[group, c] = wide[:, c * chunk : (c + 1) * chunk]
             for k in range(inner):
-                coded, steps = encode(sums_near[group, lax.rem(spot + k, inner)])
+                coded, steps = encode(sums_near[group, lax.rem(spot + k, inner)] * shrink)
                 codes_out[it, group, k] = coded
                 steps_out[it, group, k] = steps
             for k in range(1, inner):
@@ -362,22 +394,22 @@
                 near_copy(it, group, 0).start()
 
         def forward(m):
-            group = lax.rem(here + m, outer)
-            own = isinstance(m, int) and m == 0
+            group = along(outer - m)
+            own = isinstance(m, int) and m == outer
             for g in range(genes):
                 low = 1 if g == head else 0
                 awaited(steps_in.at[it, g, group, pl.ds(low, inner - low)], step_recv.at[it, g, group])
                 awaited(codes_in.at[it, g, group, pl.ds(low, inner - low)], near_recv.at[it, g, group])
                 total = sums_near[group, spot] if g == head else None
                 for k in range(low, inner):
-                    value = decode(codes_in[it, g, group, k], steps_in[it, g, group, k])
+                    value = decode(codes_in[it, g, group, k], steps_in[it, g, group, k]) * factors[g, k]
                     total = value if total is None else total + value
                 if own:
                     sums_in[it, here, g] = total
                 else:
                     sums_own[it, group, g] = total
             if not own:
-                far_copy(it, m).start()
+                far_copy(it, group).start()
 
         def reduce():
             with scope("gramwait"):
@@ -386,8 +418,13 @@
             for k in range(1, outer):
                 plane_copy(it, k).start()
             with scope("forward"):
+                for g in range(genes):
+                    low = 1 if g == head else 0
+                    awaited(lines_in.at[it, g, pl.ds(low, inner - low)], line_recv.at[it, g])
+                    for k in range(low, inner):
+                        factors[g, k] = turn_back(lines_in[it, g, k], chunk)
                 loop(1, outer, forward)
-                forward(0)
+                forward(outer)
             with scope("planewait"):
                 awaited(planes.at[it, pl.ds(0, outer - 1)], plane_recv.at[it])
             total = added(planes.at[it], outer)
@@ -456,12 +493,14 @@
         load_out[...] = load_in[...]
         drained(codes_out, near_send.at[0])
         drained(steps_out, step_send.at[0])
+        drained(lines_in.at[:, 0], line_send.at[0])
 
     @pl.when(lead)
     def _():
         drained(codes_out.at[:, :, pl.ds(1, inner - 1)], near_send.at[0])
         drained(steps_out.at[:, :, pl.ds(1, inner - 1)], step_send.at[0])
         drained(grams.at[:, pl.ds(0, inner - 1)], gram_send.at[0])
+        drained(lines_in.at[:, 0, pl.ds(1, inner - 1)], line_send.at[0])
         drained(planes.at[:, pl.ds(0, outer - 1)], plane_send.at[0])
         drained(sums_own.at[:, pl.ds(0, outer - 1)], far_send.at[0])
         drained(columns.at[pl.ds(0, outer - 1)], column_send.at[0])
@@ -487,12 +526,13 @@
     outer = cells // inner
     places = ROW_BLOCKS * gene_blocks
     dma = pltpu.SemaphoreType.DMA
-    return pl.pallas_call(
+    shapes = (
+        jax.ShapeDtypeStruct((width, cell_dev), jnp.bfloat16),
+        jax.ShapeDtypeStruct((width, chunk), jnp.float32),
+    )
+    results = pl.pallas_call(
         functools.partial(kernel, cells, inner, genes, parts),
-        out_shape=(
-            jax.ShapeDtypeStruct((width, cell_dev), jnp.bfloat16),
-            jax.ShapeDtypeStruct((width, chunk), jnp.float32),
-        ),
+        out_shape=shapes,
         in_specs=[
             pl.BlockSpec(memory_space=pltpu.SMEM),
             pl.BlockSpec(memory_space=pltpu.HBM),
@@ -520,8 +560,11 @@
             pltpu.VMEM((outer, inner, width, chunk), jnp.float32),
             pltpu.VMEM((2, outer, inner, width, chunk), jnp.int16),
             pltpu.VMEM((2, genes, outer, inner, width, chunk), jnp.int16),
-            pltpu.VMEM((2, outer, inner, 1, width), jnp.float32),
-            pltpu.VMEM((2, genes, outer, inner, 1, width), jnp.float32),
+            pltpu.VMEM((2, outer, inner, 1, chunk), jnp.float32),
+            pltpu.VMEM((2, genes, outer, inner, 1, chunk), jnp.float32),
+            pltpu.VMEM((2, 1, width), jnp.float32),
+            pltpu.VMEM((2, genes, inner, 1, width), jnp.float32),
+            pltpu.VMEM((genes, inner, width, chunk), jnp.float32),
             pltpu.VMEM((2, outer, genes, width, chunk), jnp.float32),
             pltpu.VMEM((2, outer, genes, width, chunk), jnp.float32),
             pltpu.VMEM((outer, genes, width, chunk), jnp.bfloat16),
@@ -532,7 +575,7 @@
             dma((1,)), dma((2, parts)),
             dma((1,)), dma((2,)), dma((1,)), dma((2,)), dma((1,)), dma((1,)),
             dma((1,)), dma((2, genes, outer)), dma((1,)), dma((2, genes, outer)),
-            dma((1,)), dma((2,)),
+            dma((1,)), dma((2, genes)), dma((1,)), dma((2,)),
             dma((1,)), dma((outer,)), dma((outer,)), dma((outer,)), dma((1,)), dma((1,)),
         ],
         compiler_params=pltpu.CompilerParams(
@@ -542,6 +585,25 @@
         pltpu.with_memory_space_constraint(array, pltpu.HBM)
         for array in (tile_row, tile_col, tiles[0], start_basis)
     ))
+    return pl.pallas_call(
+        deliver,
+        out_shape=shapes,
+        in_specs=[pl.BlockSpec(memory_space=pltpu.VMEM)] * 2,
+        out_specs=(pl.BlockSpec(memory_space=pl.ANY),) * 2,
+        scratch_shapes=[dma((2,))],
+        compiler_params=pltpu.CompilerParams(vmem_limit_bytes=1024 * 1024),
+    )(*results)
+
+
+def deliver(basis, load, basis_out, load_out, sems):
+    copies = [
+        pltpu.make_async_copy(basis, basis_out, sems.at[0]),
+        pltpu.make_async_copy(load, load_out, sems.at[1]),
+    ]
+    for copy in copies:
+        copy.start()
+    for copy in copies:
+        copy.wait()
 
 
 def solution(mesh):

time: 38.9 us -> 38.3 us (0.985)
  local copies, waits for them, and re-layouts: 1.27 us -> 0 us
  Pallas kernels: 36.1 us -> 36.8 us
    unnamed x2 -> x0, local copies, waits for them, and re-layouts: 1.27 us -> none
    pallas_call x0 -> x1, Pallas kernels: none -> 0.68 us  [local(): pl.pallas_call(deliver, out_shape=shapes, in_specs=[pl.BlockSpec(memory_s...]
where the time goes in v4:
time: 38.3 us; the launch traced here: 38.1 us
  Pallas kernels  36.8 us (96%)
  between operations  1.29 us (3%)
    pallas_call x1, Pallas kernels, local(): pl.pallas_call(functools.partial(kernel, cells, inner, genes, parts), out...  36.1 us

profile of v4, /device:TPU:0, one launch (start us, length us, event | category | flops | bytes accessed | tf_op | source)
XLA Modules:
  0.0 38.1 jit_solution(11149870142064511808)
XLA Ops:
  1.3 36.1 %shard_map.68 = (bf16[64,1024]{1,0:T(8,128)(2,1)S(1)}, f32[64,128]{1,0:T(8,128)S(1)}) custom-call(s32[1,1]{1,0:T(1,128)S(6)} %copy.7.slot_count, s32[1,64]{1,0:T(1,128)} %slot_row.1, s32[1,64]{1,0:T(1,128)} %slot_col.1, bf16[64,128,128]{2,1,0:T(8,128)(2,1)} %bitcast.1, bf16[64,2048]{1,0:T(8,128)(2,1)} %start.1), custom_call_target="tpu_custom_call" | custom-call | tf_op jit(solution)/shard_map/pallas_call | solution.py:533
  37.4 0.7 %shard_map.69 = (bf16[64,1024]{1,0:T(8,128)(2,1)}, f32[64,128]{1,0:T(8,128)}) custom-call(bf16[64,1024]{1,0:T(8,128)(2,1)S(1)} %get-tuple-element.4.basis, f32[64,128]{1,0:T(8,128)S(1)} %get-tuple-element.5.load), custom_call_target="tpu_custom_call" | custom-call | tf_op jit(solution)/shard_map/pallas_call | solution.py:588

commit v5 on v4

--- a/solution.py
+++ b/solution.py
@@ -100,11 +100,12 @@
     slot_count, slot_row, slot_col, tiles, start, basis_out, load_out,
     slots_in, places_out, table, held, dense, first, mine, theirs, stacked, grams, planes, factor,
     sums_near, codes_out, codes_in, steps_out, steps_in, lines_out, lines_in, factors,
-    sums_own, sums_in,
+    sums_own, far_out, far_in, fars_out, fars_in, tails_out, tails_in, gains, stretch,
     columns, middle, load_res, load_in,
     tile_sem, slot_sem, table_sem, start_sem, pair_send, pair_recv,
     gram_send, gram_recv, plane_send, plane_recv, factor_send, factor_recv,
-    near_send, near_recv, step_send, step_recv, line_send, line_recv, far_send, far_recv,
+    near_send, near_recv, step_send, step_recv, line_send, line_recv,
+    far_send, far_recv, fars_send, fars_recv, tail_send, tail_recv,
     column_send, column_recv, mid_send, mid_recv, load_send, load_recv,
 ):
     cell = lax.axis_index("cell")
@@ -192,7 +193,7 @@
     def gram_copy(it, k):
         return remote(
             grams.at[it, spot], grams.at[it, spot], gram_send.at[0], gram_recv.at[it],
-            cell=near(k),
+            cell=near(k), gene=head,
         )
 
     def plane_copy(it, k):
@@ -204,13 +205,13 @@
     def near_copy(it, group, k):
         return remote(
             codes_out.at[it, group, k], codes_in.at[it, gene, group, k],
-            near_send.at[0], near_recv.at[it, gene, group], cell=near(k), gene=head,
+            near_send.at[0], near_recv.at[gene, group], cell=near(k), gene=head,
         )
 
     def step_copy(it, group, k):
         return remote(
             steps_out.at[it, group, k], steps_in.at[it, gene, group, k],
-            step_send.at[0], step_recv.at[it, gene, group], cell=near(k), gene=head,
+            step_send.at[0], step_recv.at[gene, group], cell=near(k), gene=head,
         )
 
     def line_copy(it, k):
@@ -221,8 +222,20 @@
 
     def far_copy(it, group):
         return remote(
-            sums_own.at[it, group], sums_in.at[it, here],
+            far_out.at[it, group], far_in.at[it, here],
             far_send.at[0], far_recv.at[it], cell=group * inner + spot,
+        )
+
+    def fars_copy(it, group):
+        return remote(
+            fars_out.at[it, group], fars_in.at[it, here],
+            fars_send.at[0], fars_recv.at[it], cell=group * inner + spot,
+        )
+
+    def tail_copy(it, k):
+        return remote(
+            tails_out.at[it], tails_in.at[it, here],
+            tail_send.at[0], tail_recv.at[it], cell=far(k),
         )
 
     def column_copy(target):
@@ -367,66 +380,96 @@
             cross = sum(cross[i * width : (i + 1) * width] for i in range(it + 2))
             total = sum(cross[:, i * width : (i + 1) * width] for i in range(it + 2))
             grams[it, spot] = jnp.concatenate([total[:half], total[half:]], axis=1)
-            for k in range(1, inner):
+            for k in range(inner):
                 gram_copy(it, k).start()
+
+        def product(lanes):
+            wide = jnp.dot(
+                stacked[0 : 2 * width, :], dense[:, lanes], preferred_element_type=jnp.float32
+            )
+            return wide[:width] + wide[width:]
+
+        def dispatch(group, k, value):
+            coded, steps = encode(value * shrink)
+            codes_out[it, group, k] = coded
+            steps_out[it, group, k] = steps
+
+        def send(group, k):
+            step_copy(it, group, k).start()
+            near_copy(it, group, k).start()
 
         def multiply(m):
             group = along(outer - m)
-            wide = jnp.dot(
-                stacked[0 : 2 * width, :],
-                dense[:, pl.ds(pl.multiple_of(group * span, 128), span)],
-                preferred_element_type=jnp.float32,
-            )
-            wide = wide[:width] + wide[width:]
-            for c in range(inner):
-                sums_near[group, c] = wide[:, c * chunk : (c + 1) * chunk]
-            for k in range(inner):
-                coded, steps = encode(sums_near[group, lax.rem(spot + k, inner)] * shrink)
-                codes_out[it, group, k] = coded
-                steps_out[it, group, k] = steps
-            for k in range(1, inner):
-                step_copy(it, group, k).start()
-                near_copy(it, group, k).start()
+            if isinstance(m, int) and m == 1 and chunk % side == 0:
+                for k in list(range(1, inner)) + [0]:
+                    at = (group * inner + lax.rem(spot + k, inner)) * chunk
+                    value = product(pl.ds(pl.multiple_of(at, side), chunk))
+                    sums_near[group, lax.rem(spot + k, inner)] = value
+                    dispatch(group, k, value)
+                    if k > 0:
+                        send(group, k)
+            else:
+                wide = product(pl.ds(pl.multiple_of(group * span, 128), span))
+                for c in range(inner):
+                    sums_near[group, c] = wide[:, c * chunk : (c + 1) * chunk]
+                for k in range(inner):
+                    dispatch(group, k, sums_near[group, lax.rem(spot + k, inner)])
+                for k in range(1, inner):
+                    send(group, k)
 
             @pl.when(follow)
             def _():
-                step_copy(it, group, 0).start()
-                near_copy(it, group, 0).start()
+                send(group, 0)
 
         def forward(m):
             group = along(outer - m)
             own = isinstance(m, int) and m == outer
             for g in range(genes):
                 low = 1 if g == head else 0
-                awaited(steps_in.at[it, g, group, pl.ds(low, inner - low)], step_recv.at[it, g, group])
-                awaited(codes_in.at[it, g, group, pl.ds(low, inner - low)], near_recv.at[it, g, group])
+                awaited(steps_in.at[it, g, group, pl.ds(low, inner - low)], step_recv.at[g, group])
+                awaited(codes_in.at[it, g, group, pl.ds(low, inner - low)], near_recv.at[g, group])
                 total = sums_near[group, spot] if g == head else None
                 for k in range(low, inner):
                     value = decode(codes_in[it, g, group, k], steps_in[it, g, group, k]) * factors[g, k]
                     total = value if total is None else total + value
                 if own:
-                    sums_in[it, here, g] = total
+                    sums_own[g] = total
                 else:
-                    sums_own[it, group, g] = total
+                    coded, steps = encode(total * gains[g])
+                    far_out[it, group, g] = coded
+                    fars_out[it, group, g] = steps
             if not own:
+                fars_copy(it, group).start()
                 far_copy(it, group).start()
 
         def reduce():
+            with scope("lines"):
+                for g in range(genes):
+                    low = 1 if g == head else 0
+                    awaited(lines_in.at[it, g, pl.ds(low, inner - low)], line_recv.at[it, g])
+                    tail = lines_out[it] if g == head else None
+                    for k in range(low, inner):
+                        line = lines_in[it, g, k]
+                        tail = line if tail is None else tail + line
+                        factors[g, k] = turn_back(line, chunk)
+                    tails_out[it, g] = tail
+                    gains[g] = turn_back(1.0 / tail, chunk)
+                for k in range(1, outer):
+                    tail_copy(it, k).start()
             with scope("gramwait"):
-                awaited(grams.at[it, pl.ds(0, inner - 1)], gram_recv.at[it])
+                awaited(grams.at[it], gram_recv.at[it])
             planes[it, here] = added(grams.at[it], inner)
             for k in range(1, outer):
                 plane_copy(it, k).start()
             with scope("forward"):
-                for g in range(genes):
-                    low = 1 if g == head else 0
-                    awaited(lines_in.at[it, g, pl.ds(low, inner - low)], line_recv.at[it, g])
-                    for k in range(low, inner):
-                        factors[g, k] = turn_back(lines_in[it, g, k], chunk)
                 loop(1, outer, forward)
                 forward(outer)
             with scope("planewait"):
                 awaited(planes.at[it, pl.ds(0, outer - 1)], plane_recv.at[it])
+            awaited(tails_in.at[it, pl.ds(0, outer - 1)], tail_recv.at[it])
+            for g in range(genes):
+                for k in range(1, outer):
+                    stretch[g, k] = turn_back(tails_in[it, lax.rem(here + k, outer), g], chunk)
             total = added(planes.at[it], outer)
             total = jnp.concatenate([total[:, :width], total[:, width:]], axis=0)
             with scope("inverse"):
@@ -435,10 +478,18 @@
                 factor[...] = inverse
                 remote(factor, factor, factor_send.at[0], factor_recv.at[0], gene=other).start()
             with scope("farwait"):
-                awaited(sums_in.at[it, pl.ds(0, outer - 1)], far_recv.at[it])
+                awaited(fars_in.at[it, pl.ds(0, outer - 1)], fars_recv.at[it])
+                awaited(far_in.at[it, pl.ds(0, outer - 1)], far_recv.at[it])
             with scope("result"):
-                summed = added(sums_in.at[it], outer)
-                summed = jnp.concatenate([summed[g] for g in range(genes)], axis=1)
+                summed = []
+                for g in range(genes):
+                    part_sum = sums_own[g]
+                    for k in range(1, outer):
+                        source = lax.rem(here + k, outer)
+                        value = decode(far_in[it, source, g], fars_in[it, source, g])
+                        part_sum = part_sum + value * stretch[g, k]
+                    summed.append(part_sum)
+                summed = jnp.concatenate(summed, axis=1)
                 result = jnp.dot(
                     inverse, summed, precision=HIGH, preferred_element_type=jnp.float32
                 )
@@ -463,7 +514,7 @@
                 loop(1, outer, relay)
 
         with scope("gram"):
-            pl.when(lead)(gram)
+            pl.when(follow)(gram)
         with scope("multiply"):
             loop(1, outer + 1, multiply)
         pl.when(lead)(reduce)
@@ -493,16 +544,18 @@
         load_out[...] = load_in[...]
         drained(codes_out, near_send.at[0])
         drained(steps_out, step_send.at[0])
+        drained(grams, gram_send.at[0])
         drained(lines_in.at[:, 0], line_send.at[0])
 
     @pl.when(lead)
     def _():
         drained(codes_out.at[:, :, pl.ds(1, inner - 1)], near_send.at[0])
         drained(steps_out.at[:, :, pl.ds(1, inner - 1)], step_send.at[0])
-        drained(grams.at[:, pl.ds(0, inner - 1)], gram_send.at[0])
         drained(lines_in.at[:, 0, pl.ds(1, inner - 1)], line_send.at[0])
         drained(planes.at[:, pl.ds(0, outer - 1)], plane_send.at[0])
-        drained(sums_own.at[:, pl.ds(0, outer - 1)], far_send.at[0])
+        drained(far_in.at[:, pl.ds(0, outer - 1)], far_send.at[0])
+        drained(fars_in.at[:, pl.ds(0, outer - 1)], fars_send.at[0])
+        drained(tails_in.at[:, pl.ds(0, outer - 1)], tail_send.at[0])
         drained(columns.at[pl.ds(0, outer - 1)], column_send.at[0])
         loop(0, outer, lambda group: drained(
             middle.at[pl.ds(0, inner * genes - 1)], mid_send.at[group]
@@ -565,8 +618,15 @@
             pltpu.VMEM((2, 1, width), jnp.float32),
             pltpu.VMEM((2, genes, inner, 1, width), jnp.float32),
             pltpu.VMEM((genes, inner, width, chunk), jnp.float32),
-            pltpu.VMEM((2, outer, genes, width, chunk), jnp.float32),
-            pltpu.VMEM((2, outer, genes, width, chunk), jnp.float32),
+            pltpu.VMEM((genes, width, chunk), jnp.float32),
+            pltpu.VMEM((2, outer, genes, width, chunk), jnp.int16),
+            pltpu.VMEM((2, outer, genes, width, chunk), jnp.int16),
+            pltpu.VMEM((2, outer, genes, 1, chunk), jnp.float32),
+            pltpu.VMEM((2, outer, genes, 1, chunk), jnp.float32),
+            pltpu.VMEM((2, genes, 1, width), jnp.float32),
+            pltpu.VMEM((2, outer, genes, 1, width), jnp.float32),
+            pltpu.VMEM((genes, width, chunk), jnp.float32),
+            pltpu.VMEM((genes, outer, width, chunk), jnp.float32),
             pltpu.VMEM((outer, genes, width, chunk), jnp.bfloat16),
             pltpu.VMEM((cells, width, chunk), jnp.bfloat16),
             pltpu.VMEM((width, chunk), jnp.float32),
@@ -574,8 +634,9 @@
             dma, dma((2,)), dma, dma,
             dma((1,)), dma((2, parts)),
             dma((1,)), dma((2,)), dma((1,)), dma((2,)), dma((1,)), dma((1,)),
-            dma((1,)), dma((2, genes, outer)), dma((1,)), dma((2, genes, outer)),
-            dma((1,)), dma((2, genes)), dma((1,)), dma((2,)),
+            dma((1,)), dma((genes, outer)), dma((1,)), dma((genes, outer)),
+            dma((1,)), dma((2, genes)),
+            dma((1,)), dma((2,)), dma((1,)), dma((2,)), dma((1,)), dma((2,)),
             dma((1,)), dma((outer,)), dma((outer,)), dma((outer,)), dma((1,)), dma((1,)),
         ],
         compiler_params=pltpu.CompilerParams(

time: 38.3 us -> 36.8 us (0.961)
  Pallas kernels: 36.8 us -> 35.3 us
    pallas_call x1, Pallas kernels: 36.1 us -> 34.6 us  [local(): pl.pallas_call(functools.partial(kernel, cells, inner, genes, parts), out...]
where the time goes in v5:
time: 36.8 us; the launch traced here: 36.6 us
  Pallas kernels  35.3 us (96%)
  between operations  1.29 us (4%)
    pallas_call x1, Pallas kernels, local(): pl.pallas_call(functools.partial(kernel, cells, inner, genes, parts), out...  34.6 us

profile of v5, /device:TPU:0, one launch (start us, length us, event | category | flops | bytes accessed | tf_op | source)
XLA Modules:
  0.0 36.6 jit_solution(13621756082515994065)
XLA Ops:
  1.3 34.6 %shard_map.68 = (bf16[64,1024]{1,0:T(8,128)(2,1)S(1)}, f32[64,128]{1,0:T(8,128)S(1)}) custom-call(s32[1,1]{1,0:T(1,128)S(6)} %copy.7.slot_count, s32[1,64]{1,0:T(1,128)} %slot_row.1, s32[1,64]{1,0:T(1,128)} %slot_col.1, bf16[64,128,128]{2,1,0:T(8,128)(2,1)} %bitcast.1, bf16[64,2048]{1,0:T(8,128)(2,1)} %start.1), custom_call_target="tpu_custom_call" | custom-call | tf_op jit(solution)/shard_map/pallas_call | solution.py:586
  35.9 0.7 %shard_map.69 = (bf16[64,1024]{1,0:T(8,128)(2,1)}, f32[64,128]{1,0:T(8,128)}) custom-call(bf16[64,1024]{1,0:T(8,128)(2,1)S(1)} %get-tuple-element.4.basis, f32[64,128]{1,0:T(8,128)S(1)} %get-tuple-element.5.load), custom_call_target="tpu_custom_call" | custom-call | tf_op jit(solution)/shard_map/pallas_call | solution.py:649

commit v6 on v5

--- a/solution.py
+++ b/solution.py
@@ -8,7 +8,7 @@
 from jax.sharding import PartitionSpec as P
 
 ROW_BLOCKS = 8
-PANEL = 4
+PANEL = 8
 LEVELS = 32766.0
 MESH = pl.DeviceIdType.MESH
 HIGH = lax.Precision.HIGHEST
@@ -400,15 +400,15 @@
 
         def multiply(m):
             group = along(outer - m)
-            if isinstance(m, int) and m == 1 and chunk % side == 0:
+
+            def by_chunk():
                 for k in list(range(1, inner)) + [0]:
                     at = (group * inner + lax.rem(spot + k, inner)) * chunk
                     value = product(pl.ds(pl.multiple_of(at, side), chunk))
-                    sums_near[group, lax.rem(spot + k, inner)] = value
                     dispatch(group, k, value)
-                    if k > 0:
-                        send(group, k)
-            else:
+                    send(group, k)
+
+            def whole_group():
                 wide = product(pl.ds(pl.multiple_of(group * span, 128), span))
                 for c in range(inner):
                     sums_near[group, c] = wide[:, c * chunk : (c + 1) * chunk]
@@ -416,6 +416,16 @@
                     dispatch(group, k, sums_near[group, lax.rem(spot + k, inner)])
                 for k in range(1, inner):
                     send(group, k)
+
+            if isinstance(m, int) and m == 1 and chunk % side == 0:
+                pl.when(follow)(by_chunk)
+
+                @pl.when(lead)
+                def _():
+                    whole_group()
+
+                return
+            whole_group()
 
             @pl.when(follow)
             def _():

time: 36.8 us -> 36.5 us (level)
  no operation moved by 1% of the time
where the time goes in v6:
time: 36.5 us; the launch traced here: 36.3 us
  Pallas kernels  35 us (96%)
  between operations  1.29 us (4%)
    pallas_call x1, Pallas kernels, local(): pl.pallas_call(functools.partial(kernel, cells, inner, genes, parts), out...  34.3 us

profile of v6, /device:TPU:0, one launch (start us, length us, event | category | flops | bytes accessed | tf_op | source)
XLA Modules:
  0.0 36.3 jit_solution(13486551799283624171)
XLA Ops:
  1.3 34.3 %shard_map.68 = (bf16[64,1024]{1,0:T(8,128)(2,1)S(1)}, f32[64,128]{1,0:T(8,128)S(1)}) custom-call(s32[1,1]{1,0:T(1,128)S(6)} %copy.7.slot_count, s32[1,64]{1,0:T(1,128)} %slot_row.1, s32[1,64]{1,0:T(1,128)} %slot_col.1, bf16[64,128,128]{2,1,0:T(8,128)(2,1)} %bitcast.1, bf16[64,2048]{1,0:T(8,128)(2,1)} %start.1), custom_call_target="tpu_custom_call" | custom-call | tf_op jit(solution)/shard_map/pallas_call | solution.py:596
  35.6 0.7 %shard_map.69 = (bf16[64,1024]{1,0:T(8,128)(2,1)}, f32[64,128]{1,0:T(8,128)}) custom-call(bf16[64,1024]{1,0:T(8,128)(2,1)S(1)} %get-tuple-element.4.basis, f32[64,128]{1,0:T(8,128)S(1)} %get-tuple-element.5.load), custom_call_target="tpu_custom_call" | custom-call | tf_op jit(solution)/shard_map/pallas_call | solution.py:659

commit v7 on v6

--- a/solution.py
+++ b/solution.py
@@ -293,7 +293,7 @@
         )
 
     def first_scores():
-        stages = 4
+        stages = 8
         share_cols = gene_blocks // stages
         with scope("place"):
             place(0, share_cols)
@@ -474,12 +474,12 @@
             with scope("forward"):
                 loop(1, outer, forward)
                 forward(outer)
-            with scope("planewait"):
-                awaited(planes.at[it, pl.ds(0, outer - 1)], plane_recv.at[it])
             awaited(tails_in.at[it, pl.ds(0, outer - 1)], tail_recv.at[it])
             for g in range(genes):
                 for k in range(1, outer):
                     stretch[g, k] = turn_back(tails_in[it, lax.rem(here + k, outer), g], chunk)
+            with scope("planewait"):
+                awaited(planes.at[it, pl.ds(0, outer - 1)], plane_recv.at[it])
             total = added(planes.at[it], outer)
             total = jnp.concatenate([total[:, :width], total[:, width:]], axis=0)
             with scope("inverse"):

time: 36.5 us -> 36.3 us (level)
  no operation moved by 1% of the time
where the time goes in v7:
time: 36.3 us; the launch traced here: 36.1 us
  Pallas kernels  34.9 us (96%)
  between operations  1.29 us (4%)
    pallas_call x1, Pallas kernels, local(): pl.pallas_call(functools.partial(kernel, cells, inner, genes, parts), out...  34.2 us

profile of v7, /device:TPU:0, one launch (start us, length us, event | category | flops | bytes accessed | tf_op | source)
XLA Modules:
  0.0 36.1 jit_solution(2311334916544146085)
XLA Ops:
  1.3 34.2 %shard_map.68 = (bf16[64,1024]{1,0:T(8,128)(2,1)S(1)}, f32[64,128]{1,0:T(8,128)S(1)}) custom-call(s32[1,1]{1,0:T(1,128)S(6)} %copy.7.slot_count, s32[1,64]{1,0:T(1,128)} %slot_row.1, s32[1,64]{1,0:T(1,128)} %slot_col.1, bf16[64,128,128]{2,1,0:T(8,128)(2,1)} %bitcast.1, bf16[64,2048]{1,0:T(8,128)(2,1)} %start.1), custom_call_target="tpu_custom_call" | custom-call | tf_op jit(solution)/shard_map/pallas_call | solution.py:596
  35.5 0.7 %shard_map.69 = (bf16[64,1024]{1,0:T(8,128)(2,1)}, f32[64,128]{1,0:T(8,128)}) custom-call(bf16[64,1024]{1,0:T(8,128)(2,1)S(1)} %get-tuple-element.4.basis, f32[64,128]{1,0:T(8,128)S(1)} %get-tuple-element.5.load), custom_call_target="tpu_custom_call" | custom-call | tf_op jit(solution)/shard_map/pallas_call | solution.py:659
